TPU v7x, 32 devices: a 4x4x1 block of a 4x4x8 slice. The times are simulated.
32 devices in a mesh: rep: 1 (over z), dp: 32 (over x, y, core).
Axes of the slice: x: 4, y: 4, z: 1, core: 2. Of those that a mesh axis runs over, the one named last changes fastest.
The devices are a block of a 4x4x8 slice.
Arguments:
- x: bfloat16 [32, 2048, 512], P(('rep', 'dp'))
- dy: bfloat16 [32, 2048, 512], P(('rep', 'dp'))
- w_gate: bfloat16 [2, 512, 3072], P(None, 'dp')
- w_up: bfloat16 [2, 512, 3072], P(None, 'dp')
- w_down: bfloat16 [2, 3072, 512], P(None, 'dp')
- m_w_gate: float32 [2, 512, 3072], P(None, 'dp')
- m_w_up: float32 [2, 512, 3072], P(None, 'dp')
- m_w_down: float32 [2, 3072, 512], P(None, 'dp')
- v_w_gate: float32 [2, 512, 3072], P(None, 'dp')
- v_w_up: float32 [2, 512, 3072], P(None, 'dp')
- v_w_down: float32 [2, 3072, 512], P(None, 'dp')
Outputs:
- output 1: bfloat16 [2, 512, 3072], P('rep', 'dp')
- output 2: bfloat16 [2, 512, 3072], P('rep', 'dp')
- output 3: bfloat16 [2, 3072, 512], P('rep', 'dp')
- output 4: float32 [2, 512, 3072], P('rep', 'dp')
- output 5: float32 [2, 512, 3072], P('rep', 'dp')
- output 6: float32 [2, 3072, 512], P('rep', 'dp')
- output 7: float32 [2, 512, 3072], P('rep', 'dp')
- output 8: float32 [2, 512, 3072], P('rep', 'dp')
- output 9: float32 [2, 3072, 512], P('rep', 'dp')
All inputs are finite; a program needn't handle non-finite values.
Results may differ from a plain program's by a relative error of at most 0.022.
Values are sent between devices in bfloat16 or wider.
A program may use at most 768 MiB of HBM per device.

v0:
```python
import jax
import jax.numpy as jnp
from jax import lax
from jax.sharding import PartitionSpec as P

NAMES = ("w_gate", "w_up", "w_down")


def matmul(a, w):
    return jnp.dot(a, w, preferred_element_type=jnp.float32).astype(jnp.bfloat16)


def normed(h):
    wide = h.astype(jnp.float32)
    scale = lax.rsqrt(jnp.mean(wide**2, -1, keepdims=True) + 1e-6)
    return (wide * scale).astype(jnp.bfloat16)


def layer(h, w):
    a = normed(h)
    gate = jnp.dot(a, w["w_gate"], preferred_element_type=jnp.float32)
    up = jnp.dot(a, w["w_up"], preferred_element_type=jnp.float32)
    return h + matmul((jax.nn.silu(gate) * up).astype(jnp.bfloat16), w["w_down"])


def adamw(w, m, v, g):
    m = 0.9 * m + 0.1 * g
    v = 0.95 * v + 0.05 * g * g
    step = m * lax.rsqrt(v + 1e-8) + 0.1 * w
    return (w - 0.02 * step).astype(jnp.bfloat16), m, v


def clipped(gradients, sum_of_squares, count):
    factor = jnp.minimum(1.0, 0.5 * lax.rsqrt(sum_of_squares / count + 1e-30))
    return [g * factor for g in gradients]


def solution(mesh):
    def fetched(weights, number):
        return {name: lax.all_gather(w[number], "dp", axis=0, tiled=True) for name, w in zip(NAMES, weights, strict=True)}

    def step(x, dy, *arrays):
        weights, m, v = (arrays[i : i + 3] for i in (0, 3, 6))
        layers = weights[0].shape[0]
        h, kept = x[0], []
        for number in range(layers):
            kept.append(h)
            h = layer(h, fetched(weights, number))
        by_h, mine = dy[0], [None] * layers
        for number in reversed(range(layers)):
            _, back = jax.vjp(lambda w, h: layer(h, w), fetched(weights, number), kept[number])
            by_w, by_h = back(by_h)
            mine[number] = [lax.psum_scatter(by_w[name], "dp", scatter_dimension=0, tiled=True) for name in NAMES]
        gradients = [jnp.stack([mine[number][i] for number in range(layers)]).astype(jnp.float32) for i in range(3)]
        squares = lax.psum(sum(jnp.sum(g * g) for g in gradients), "dp")
        gradients = clipped(gradients, squares, lax.psum(1, "dp") * sum(g.size for g in gradients))
        new = [adamw(w.astype(jnp.float32), m, v, g) for w, m, v, g in zip(weights, m, v, gradients, strict=True)]
        return tuple(one[which] for which in range(3) for one in new)

    states, cut = P(("rep", "dp"), None, None), P(None, "dp", None)
    return jax.shard_map(
        step,
        mesh=mesh,
        in_specs=(states, states) + (cut,) * 9,
        out_specs=(P("rep", "dp", None),) * 9,
        check_vma=False,
    )
```

profile of v0, /device:TPU:97, one launch (start us, length us, event | category | flops | bytes accessed | tf_op | source)
XLA Modules:
  0.0 847.8 jit_solution(17894867536778962538)
XLA Ops:
  14.5 2.9 copy.20
  17.9 4.2 copy.21
  22.1 32.6 %all-gather.13.cloned.1.call-done = bf16[1,512,3072]{2,1,0:T(8,128)(2,1)} async-done(((bf16[1,16,3072]{2,1,0:T(8,128)(2,1)}), bf16[1,512,3072]{2,1,0:T(8,128)(2,1)}) %all-gather.13.cloned.1.call-update) | async-done | bytes 3145744 | tf_op jit(solution)/shard_map/all_gather | solution.py:40
  54.8 13.6 %fusion.42 = f32[2048,3072]{1,0:T(8,128)} fusion(bf16[1,512,3072]{2,1,0:T(8,128)(2,1)} %all-gather.13.cloned.1.call-done, bf16[1,2048,512]{1,2,0:T(8,128)(2,1)S(1)} %copy.20, f32[2048]{0:T(1024)S(1)} %add_rsqrt_fusion), kind=kOutput, calls=%fused_computation.59 | convolution fusion | flops 6445596672 | bytes 30416896 | tf_op jit(solution)/shard_map/dot_general | solution.py:21
  68.4 28.1 %all-gather.15.cloned.1.call-done = bf16[1,512,3072]{2,1,0:T(8,128)(2,1)} async-done(((bf16[1,16,3072]{2,1,0:T(8,128)(2,1)}), bf16[1,512,3072]{2,1,0:T(8,128)(2,1)}) %all-gather.15.cloned.1.call-update) | async-done | bytes 3145744 | tf_op jit(solution)/shard_map/all_gather | solution.py:40
  96.5 24.1 %multiply_convert_fusion.1 = (bf16[2048,3072]{1,0:T(8,128)(2,1)}, f32[2048,3072]{1,0:T(8,128)}) fusion(f32[2048,3072]{1,0:T(8,128)} %fusion.42, bf16[1,512,3072]{2,1,0:T(8,128)(2,1)} %all-gather.15.cloned.1.call-done, bf16[1,2048,512]{1,2,0:T(8,128)(2,1)S(1)} %copy.20, f32[2048]{0:T(1024)S(1)} %add_rsqrt_fusion), kind=kOutput, calls=%fused_computation.17 | convolution fusion | flops 6483345408 | bytes 68165632 | tf_op jit(solution)/shard_map/dot_general | solution.py:22
  120.6 17.7 %all-gather.17.cloned.1.call-done = bf16[1,3072,512]{2,1,0:T(8,128)(2,1)} async-done(((bf16[1,96,512]{2,1,0:T(8,128)(2,1)}), bf16[1,3072,512]{2,1,0:T(8,128)(2,1)}) %all-gather.17.cloned.1.call-update) | async-done | bytes 3145744 | tf_op jit(solution)/shard_map/all_gather | solution.py:40
  138.3 11.8 %fusion.26 = (f32[2048]{0:T(1024)S(1)}, bf16[2048,512]{0,1:T(8,128)(2,1)}) fusion(bf16[2048,3072]{1,0:T(8,128)(2,1)} %get-tuple-element.24, bf16[1,3072,512]{2,1,0:T(8,128)(2,1)} %all-gather.17.cloned.1.call-done, bf16[1,2048,512]{1,2,0:T(8,128)(2,1)S(1)} %copy.20), kind=kOutput, calls=%fused_computation.43 | convolution fusion | flops 6447691776 | bytes 19931136 | tf_op jit(solution)/shard_map/dot_general | solution.py:10
  150.1 29.8 %all-gather.21.cloned.1.call-done = bf16[1,3072,512]{2,1,0:T(8,128)(2,1)} async-done(((bf16[1,96,512]{2,1,0:T(8,128)(2,1)}), bf16[1,3072,512]{2,1,0:T(8,128)(2,1)}) %all-gather.21.cloned.1.call-update) | async-done | bytes 3145744 | tf_op jit(solution)/shard_map/all_gather | solution.py:40
  180.0 12.3 %convolution_convert_fusion.1 = bf16[2048,3072]{1,0:T(8,128)(2,1)} fusion(bf16[1,3072,512]{2,1,0:T(8,128)(2,1)} %all-gather.21.cloned.1.call-done, bf16[1,2048,512]{2,1,0:T(8,128)(2,1)} %param.12), kind=kOutput, calls=%fused_computation.25 | convolution fusion | flops 6448742400 | bytes 17825792 | tf_op jit(solution)/shard_map/transpose(jvp())/dot_general | solution.py:10
  192.2 29.4 %all-gather.23.cloned.1.call-done = bf16[1,512,3072]{2,1,0:T(8,128)(2,1)} async-done(((bf16[1,16,3072]{2,1,0:T(8,128)(2,1)}), bf16[1,512,3072]{2,1,0:T(8,128)(2,1)}) %all-gather.23.cloned.1.call-update) | async-done | bytes 3145744 | tf_op jit(solution)/shard_map/all_gather | solution.py:40
  221.6 13.7 %fusion.29 = f32[2048,3072]{1,0:T(8,128)} fusion(bf16[1,512,3072]{2,1,0:T(8,128)(2,1)} %all-gather.23.cloned.1.call-done, bf16[2048,512]{0,1:T(8,128)(2,1)S(1)} %copy-done.4, f32[2048]{0:T(1024)S(1)} %fusion.91), kind=kOutput, calls=%fused_computation.46 | convolution fusion | flops 6445596672 | bytes 30416896 | tf_op jit(solution)/shard_map/jvp()/dot_general | solution.py:22
  235.3 27.9 %all-gather.19.cloned.1.call-done = bf16[1,512,3072]{2,1,0:T(8,128)(2,1)} async-done(((bf16[1,16,3072]{2,1,0:T(8,128)(2,1)}), bf16[1,512,3072]{2,1,0:T(8,128)(2,1)}) %all-gather.19.cloned.1.call-update) | async-done | bytes 3145744 | tf_op jit(solution)/shard_map/all_gather | solution.py:40
  263.2 29.9 %fusion.2 = (bf16[2048,3072]{1,0:T(8,128)(2,1)}, f32[2048,3072]{1,0:T(8,128)}) fusion(f32[2048,3072]{1,0:T(8,128)} %fusion.29, bf16[2048,3072]{1,0:T(8,128)(2,1)} %convolution_convert_fusion.1, bf16[1,512,3072]{2,1,0:T(8,128)(2,1)} %all-gather.19.cloned.1.call-done, bf16[2048,512]{0,1:T(8,128)(2,1)S(1)} %copy-done.4, f32[2048]{0:T(1024)S(1)} %fusion.91), kind=kOutput, calls=%fused_computation.8 | convolution fusion | flops 6521094144 | bytes 80748544 | tf_op jit(solution)/shard_map/jvp()/dot_general | solution.py:21
  293.1 18.1 %fusion.50 = bf16[2048,512]{0,1:T(8,128)(2,1)} fusion(bf16[1,512,3072]{2,1,0:T(8,128)(2,1)} %all-gather.23.cloned.1.call-done, bf16[2048,3072]{1,0:T(8,128)(2,1)} %convolution_convert_fusion.1, f32[2048,3072]{1,0:T(8,128)} %get-tuple-element.29), kind=kOutput, calls=%fused_computation.63 | convolution fusion | flops 6481248256 | bytes 42991616 | tf_op jit(solution)/shard_map/transpose(jvp())/dot_general | solution.py:22
  311.3 11.4 %fusion.28 = (f32[2048]{0:T(1024)S(1)}, bf16[2048,512]{0,1:T(8,128)(2,1)S(1)}) fusion(bf16[2048,512]{0,1:T(8,128)(2,1)S(1)} %copy-done.4, bf16[2048,512]{0,1:T(8,128)(2,1)} %fusion.50, bf16[2048,3072]{1,0:T(8,128)(2,1)} %get-tuple-element.28, bf16[1,512,3072]{2,1,0:T(8,128)(2,1)} %all-gather.19.cloned.1.call-done), kind=kOutput, calls=%fused_computation.45 | convolution fusion | flops 6447691776 | bytes 22028288 | tf_op jit(solution)/shard_map/transpose(jvp())/dot_general | solution.py:21
  325.4 11.3 %convolution_convert_fusion.2 = bf16[3072,512]{1,0:T(8,128)(2,1)} fusion(bf16[2048,3072]{1,0:T(8,128)(2,1)} %get-tuple-element.24, bf16[2048,512]{0,1:T(8,128)(2,1)S(1)} %fusion.59), kind=kOutput, calls=%fused_computation.36 | convolution fusion | flops 6444023808 | bytes 17825792 | tf_op jit(solution)/shard_map/transpose(jvp())/dot_general | solution.py:10
  336.9 19.7 %fusion.15 = bf16[3072,512]{1,0:T(8,128)(2,1)} fusion(f32[2048,3072]{1,0:T(8,128)} %fusion.29, bf16[1,2048,512]{2,1,0:T(8,128)(2,1)S(1)} %copy-done.3, f32[2048,3072]{1,0:T(8,128)} %get-tuple-element.29), kind=kOutput, calls=%fused_computation.33 | convolution fusion | flops 6481772544 | bytes 55574528 | tf_op jit(solution)/shard_map/transpose(jvp())/dot_general | solution.py:10
  356.8 11.9 %convolution_convert_fusion = bf16[2048,3072]{1,0:T(8,128)(2,1)} fusion(bf16[2048,512]{0,1:T(8,128)(2,1)} %copy-done.5, bf16[1,3072,512]{2,1,0:T(8,128)(2,1)} %all-gather.17.cloned.1.call-done), kind=kOutput, calls=%fused_computation.24 | convolution fusion | flops 6448742400 | bytes 17825792 | tf_op jit(solution)/shard_map/transpose(jvp())/dot_general | solution.py:10
  368.7 17.2 %fusion.17 = bf16[512,3072]{1,0:T(8,128)(2,1)} fusion(bf16[2048,3072]{1,0:T(8,128)(2,1)} %convolution_convert_fusion, f32[2048,3072]{1,0:T(8,128)} %fusion.42, bf16[1,2048,512]{1,2,0:T(8,128)(2,1)S(1)} %copy-done.1, f32[2048]{0:T(1024)S(1)} %copy-done.16), kind=kOutput, calls=%fused_computation.35 | convolution fusion | flops 6484918272 | bytes 42999808 | tf_op jit(solution)/shard_map/transpose(jvp())/dot_general | solution.py:22
  386.0 18.2 %fusion.16 = bf16[512,3072]{1,0:T(8,128)(2,1)} fusion(bf16[2048,3072]{1,0:T(8,128)(2,1)} %convolution_convert_fusion.1, bf16[2048,512]{0,1:T(8,128)(2,1)} %get-tuple-element.27, f32[2048]{0:T(1024)S(1)} %fusion.91, f32[2048,3072]{1,0:T(8,128)} %get-tuple-element.29), kind=kOutput, calls=%fused_computation.34 | convolution fusion | flops 6484918272 | bytes 42999808 | tf_op jit(solution)/shard_map/transpose(jvp())/dot_general | solution.py:22
  404.4 24.9 %fusion.18 = bf16[512,3072]{1,0:T(8,128)(2,1)} fusion(f32[2048,3072]{1,0:T(8,128)} %fusion.42, f32[2048,3072]{1,0:T(8,128)} %get-tuple-element.25, bf16[2048,3072]{1,0:T(8,128)(2,1)} %convolution_convert_fusion, bf16[1,2048,512]{1,2,0:T(8,128)(2,1)S(1)} %copy-done.1, f32[2048]{0:T(1024)S(1)} %copy-done.16), kind=kOutput, calls=%fused_computation.38 | convolution fusion | flops 6516375552 | bytes 68165632 | tf_op jit(solution)/shard_map/transpose(jvp())/dot_general | solution.py:21
  429.4 13.0 %convolution_convert_fusion.3 = bf16[512,3072]{1,0:T(8,128)(2,1)} fusion(bf16[2048,3072]{1,0:T(8,128)(2,1)} %get-tuple-element.28, bf16[2048,512]{0,1:T(8,128)(2,1)} %get-tuple-element.27, f32[2048]{0:T(1024)S(1)} %fusion.91), kind=kOutput, calls=%fused_computation.37 | convolution fusion | flops 6445596672 | bytes 17833984 | tf_op jit(solution)/shard_map/transpose(jvp())/dot_general | solution.py:21
  442.5 40.4 %reduce-scatter.17.cloned.1.call-done = bf16[96,512]{1,0:T(8,128)(2,1)} async-done(((bf16[3072,512]{1,0:T(8,128)(2,1)}), bf16[96,512]{1,0:T(8,128)(2,1)}) %reduce-scatter.17.cloned.1.call-update) | async-done | bytes 98320 | tf_op jit(solution)/shard_map/reduce_scatter | solution.py:53
  482.9 1.6 fusion.81
  484.6 74.1 %reduce-scatter.11.cloned.1.call-done = bf16[16,3072]{1,0:T(8,128)(2,1)} async-done(((bf16[512,3072]{1,0:T(8,128)(2,1)}), bf16[16,3072]{1,0:T(8,128)(2,1)}) %reduce-scatter.11.cloned.1.call-update) | async-done | bytes 98320 | tf_op jit(solution)/shard_map/reduce_scatter | solution.py:53
  558.6 75.5 %reduce-scatter.13.cloned.1.call-done = bf16[16,3072]{1,0:T(8,128)(2,1)} async-done(((bf16[512,3072]{1,0:T(8,128)(2,1)}), bf16[16,3072]{1,0:T(8,128)(2,1)}) %reduce-scatter.13.cloned.1.call-update) | async-done | bytes 98320 | tf_op jit(solution)/shard_map/reduce_scatter | solution.py:53
  635.8 74.0 %reduce-scatter.7.cloned.1.call-done = bf16[16,3072]{1,0:T(8,128)(2,1)} async-done(((bf16[512,3072]{1,0:T(8,128)(2,1)}), bf16[16,3072]{1,0:T(8,128)(2,1)}) %reduce-scatter.7.cloned.1.call-update) | async-done | bytes 98320 | tf_op jit(solution)/shard_map/reduce_scatter | solution.py:53
  709.8 75.6 %reduce-scatter.9.cloned.1.call-done = bf16[16,3072]{1,0:T(8,128)(2,1)} async-done(((bf16[512,3072]{1,0:T(8,128)(2,1)}), bf16[16,3072]{1,0:T(8,128)(2,1)}) %reduce-scatter.9.cloned.1.call-update) | async-done | bytes 98320 | tf_op jit(solution)/shard_map/reduce_scatter | solution.py:53
  789.0 46.2 %psum.7 = f32[]{:T(128)} all-reduce(f32[]{:T(128)S(6)} %add.99), channel_id=1, replica_groups=mesh['rep'=1,'dp'=32] {'dp'}, use_global_device_ids=true, to_apply=%region_12.13 | all-reduce | flops 1 | bytes 8 | tf_op jit(solution)/shard_map/psum | solution.py:55
  836.0 2.0 fusion.87
  838.0 2.5 fusion.78
  (69 shorter events, 14.4 us)
Async XLA Ops:
  7.2 47.6 %all-gather.13.cloned.1.call-start = ((), (), s32[]{:S(2)}) async-start(), calls=%async_computation.12 | async-start | bytes 3244032 | tf_op jit(solution)/shard_map/all_gather | solution.py:40
  8.9 87.6 %all-gather.15.cloned.1.call-start = ((), (), s32[]{:S(2)}) async-start(), calls=%async_computation.13 | async-start | bytes 3244032 | tf_op jit(solution)/shard_map/all_gather | solution.py:40
  10.7 127.6 %all-gather.17.cloned.1.call-start = ((), (), s32[]{:S(2)}) async-start(), calls=%async_computation.14 | async-start | bytes 3244032 | tf_op jit(solution)/shard_map/all_gather | solution.py:40
  12.5 167.5 %all-gather.21.cloned.1.call-start = ((), (), s32[]{:S(2)}) async-start(), calls=%async_computation.16 | async-start | bytes 3244032 | tf_op jit(solution)/shard_map/all_gather | solution.py:40
  13.1 208.5 %all-gather.23.cloned.1.call-start = ((), (), s32[]{:S(2)}) async-start(), calls=%async_computation.17 | async-start | bytes 3244032 | tf_op jit(solution)/shard_map/all_gather | solution.py:40
  13.8 249.5 %all-gather.19.cloned.1.call-start = ((), (), s32[]{:S(2)}) async-start(), calls=%async_computation.15 | async-start | bytes 3244032 | tf_op jit(solution)/shard_map/all_gather | solution.py:40
  14.4 428.1 %reduce-scatter.15.cloned.1.call-start = ((), (), s32[]{:S(2)}) async-start(), calls=%async_computation.10 | async-start | bytes 3244032 | tf_op jit(solution)/shard_map/reduce_scatter | solution.py:53
  17.4 120.9 %copy-start = (bf16[1,2048,512]{1,2,0:T(8,128)(2,1)}, bf16[1,2048,512]{1,2,0:T(8,128)(2,1)S(1)}, u32[]{:S(2)}) copy-start(bf16[1,2048,512]{1,2,0:T(8,128)(2,1)S(1)} %copy.20) | copy-start | bytes 6291460
  17.9 78.7 %copy-start.15 = (f32[2048]{0:T(1024)}, f32[2048]{0:T(1024)S(1)}, u32[]{:S(2)}) copy-start(f32[2048]{0:T(1024)S(1)} %add_rsqrt_fusion) | copy-start | bytes 24580
  150.1 71.5 %copy-start.4 = (bf16[2048,512]{0,1:T(8,128)(2,1)S(1)}, bf16[2048,512]{0,1:T(8,128)(2,1)}, u32[]{:S(2)}) copy-start(bf16[2048,512]{0,1:T(8,128)(2,1)} %get-tuple-element.27) | copy-start | bytes 6291460
  311.3 11.4 %copy-start.2 = (bf16[1,2048,512]{1,2,0:T(8,128)(2,1)S(1)}, bf16[1,2048,512]{1,2,0:T(8,128)(2,1)}, u32[]{:S(2)}) copy-start(bf16[1,2048,512]{1,2,0:T(8,128)(2,1)} %copy.21) | copy-start | bytes 6291460
  324.1 1.3 copy-start.5
  325.4 11.5 %copy-start.3 = (bf16[1,2048,512]{2,1,0:T(8,128)(2,1)S(1)}, bf16[1,2048,512]{2,1,0:T(8,128)(2,1)}, u32[]{:S(2)}) copy-start(bf16[1,2048,512]{2,1,0:T(8,128)(2,1)} %param.12) | copy-start | bytes 6291460
  336.8 146.1 %reduce-scatter.17.cloned.1.call-start = ((), (), s32[]{:S(2)}) async-start(), calls=%async_computation.11 | async-start | bytes 3244032 | tf_op jit(solution)/shard_map/reduce_scatter | solution.py:53
  356.7 12.0 %copy-start.1 = (bf16[1,2048,512]{1,2,0:T(8,128)(2,1)S(1)}, bf16[1,2048,512]{1,2,0:T(8,128)(2,1)}, u32[]{:S(2)}) copy-start(bf16[1,2048,512]{1,2,0:T(8,128)(2,1)} %copy-done) | copy-start | bytes 6291460
  356.7 12.0 %copy-start.16 = (f32[2048]{0:T(1024)S(1)}, f32[2048]{0:T(1024)}, u32[]{:S(2)}) copy-start(f32[2048]{0:T(1024)} %copy-done.15) | copy-start | bytes 24580
  356.7 202.0 %reduce-scatter.11.cloned.1.call-start = ((), (), s32[]{:S(2)}) async-start(), calls=%async_computation.8 | async-start | bytes 3244032 | tf_op jit(solution)/shard_map/reduce_scatter | solution.py:53
  385.9 248.2 %reduce-scatter.13.cloned.1.call-start = ((), (), s32[]{:S(2)}) async-start(), calls=%async_computation.9 | async-start | bytes 3244032 | tf_op jit(solution)/shard_map/reduce_scatter | solution.py:53
  404.3 305.6 %reduce-scatter.7.cloned.1.call-start = ((), (), s32[]{:S(2)}) async-start(), calls=%async_computation.6 | async-start | bytes 3244032 | tf_op jit(solution)/shard_map/reduce_scatter | solution.py:53
  429.3 406.7 %copy-start.8 = (bf16[2,96,512]{2,1,0:T(8,128)(2,1)S(1)}, bf16[2,96,512]{2,1,0:T(8,128)(2,1)}, u32[]{:S(2)}) copy-start(bf16[2,96,512]{2,1,0:T(8,128)(2,1)} %param.15) | copy-start | bytes 589828
  429.3 406.6 %copy-start.9 = (f32[2,96,512]{2,1,0:T(8,128)S(1)}, f32[2,96,512]{2,1,0:T(8,128)}, u32[]{:S(2)}) copy-start(f32[2,96,512]{2,1,0:T(8,128)} %param.21) | copy-start | bytes 1179652
  429.3 406.6 %copy-start.10 = (f32[2,96,512]{2,1,0:T(8,128)S(1)}, f32[2,96,512]{2,1,0:T(8,128)}, u32[]{:S(2)}) copy-start(f32[2,96,512]{2,1,0:T(8,128)} %param.18) | copy-start | bytes 1179652
  429.3 356.1 %reduce-scatter.9.cloned.1.call-start = ((), (), s32[]{:S(2)}) async-start(), calls=%async_computation.7 | async-start | bytes 3244032 | tf_op jit(solution)/shard_map/reduce_scatter | solution.py:53
  442.4 395.6 %copy-start.6 = (bf16[2,16,3072]{2,1,0:T(8,128)(2,1)S(1)}, bf16[2,16,3072]{2,1,0:T(8,128)(2,1)}, u32[]{:S(2)}) copy-start(bf16[2,16,3072]{2,1,0:T(8,128)(2,1)} %param.13) | copy-start | bytes 589828
  442.4 395.6 %copy-start.7 = (bf16[2,16,3072]{2,1,0:T(8,128)(2,1)S(1)}, bf16[2,16,3072]{2,1,0:T(8,128)(2,1)}, u32[]{:S(2)}) copy-start(bf16[2,16,3072]{2,1,0:T(8,128)(2,1)} %param.14) | copy-start | bytes 589828
  442.4 395.6 %copy-start.11 = (f32[2,16,3072]{2,1,0:T(8,128)S(1)}, f32[2,16,3072]{2,1,0:T(8,128)}, u32[]{:S(2)}) copy-start(f32[2,16,3072]{2,1,0:T(8,128)} %param.19) | copy-start | bytes 1179652
  442.4 395.6 %copy-start.12 = (f32[2,16,3072]{2,1,0:T(8,128)S(1)}, f32[2,16,3072]{2,1,0:T(8,128)}, u32[]{:S(2)}) copy-start(f32[2,16,3072]{2,1,0:T(8,128)} %param.16) | copy-start | bytes 1179652
  442.4 395.6 %copy-start.13 = (f32[2,16,3072]{2,1,0:T(8,128)S(1)}, f32[2,16,3072]{2,1,0:T(8,128)}, u32[]{:S(2)}) copy-start(f32[2,16,3072]{2,1,0:T(8,128)} %param.20) | copy-start | bytes 1179652
  442.4 395.5 %copy-start.14 = (f32[2,16,3072]{2,1,0:T(8,128)S(1)}, f32[2,16,3072]{2,1,0:T(8,128)}, u32[]{:S(2)}) copy-start(f32[2,16,3072]{2,1,0:T(8,128)} %param.17) | copy-start | bytes 1179652
Sparse Core Ops, SparseCore 0:
  10.7 44.0 all-gather.12
  57.4 39.0 all-gather.14
  99.2 39.0 all-gather.16
  140.8 39.0 all-gather.20
  182.5 39.0 all-gather.22
  224.1 39.0 all-gather.18
  336.9 70.1 reduce-scatter.14
  410.6 72.2 reduce-scatter.16
  486.4 72.2 reduce-scatter.10
  561.9 72.1 reduce-scatter.12
  637.6 72.1 reduce-scatter.6
  713.2 72.2 reduce-scatter.8
where the time goes:
time: 857 us; the launch traced here: 848 us
  waiting for transfers between devices  507 us (59%)
  matrix products  251 us (29%)
  blocking collectives  46.2 us (5%)
  between operations  17.5 us (2%)
  local copies, waits for them, and re-layouts  13.5 us (2%)
  other arithmetic  11.3 us (1%)
    reduce_scatter x6, waiting for transfers between devices, step(): lax.psum_scatter(by_w[name], 'dp', scatter_dimension=0, tiled=True)  340 us
    all_gather x6, waiting for transfers between devices, fetched(): lax.all_gather(w[number], 'dp', axis=0, tiled=True)  166 us
    dot_general x5, matrix products, layer(): gate = jnp.dot(a, w['w_gate'], preferred_element_type=jnp.float32)  92.8 us
    dot_general x5, matrix products, layer(): up = jnp.dot(a, w['w_up'], preferred_element_type=jnp.float32)  91.3 us
    dot_general x5, matrix products, matmul(): jnp.dot(a, w, preferred_element_type=jnp.float32).astype(jnp.bfloat16)  67 us
    psum x1, blocking collectives, step(): squares = lax.psum(sum((jnp.sum(g * g) for g in gradients)), 'dp')  46.2 us
  transfers between devices with their start and end apart: 12, of which 11 were waited for; matrix products, arithmetic and copies ran while one was open for 23% of the time, Pallas kernels for 0%

commit v1 on v0

v1 whole, which is shorter than its diff:
```python
import functools
import math

import jax
import jax.numpy as jnp
from jax import lax
from jax.experimental import pallas as pl
from jax.experimental.pallas import tpu as pltpu
from jax.sharding import PartitionSpec as P

NAMES = ("w_gate", "w_up", "w_down")
MESH = pl.DeviceIdType.MESH
CORES = 2
VMEM = pl.BlockSpec(memory_space=pltpu.VMEM)
HBM = pl.BlockSpec(memory_space=pl.ANY)


def matmul(a, w):
    return jnp.dot(a, w, preferred_element_type=jnp.float32).astype(jnp.bfloat16)


def normed(h):
    wide = h.astype(jnp.float32)
    scale = lax.rsqrt(jnp.mean(wide**2, -1, keepdims=True) + 1e-6)
    return (wide * scale).astype(jnp.bfloat16)


def layer(h, w):
    a = normed(h)
    gate = jnp.dot(a, w["w_gate"], preferred_element_type=jnp.float32)
    up = jnp.dot(a, w["w_up"], preferred_element_type=jnp.float32)
    return h + matmul((jax.nn.silu(gate) * up).astype(jnp.bfloat16), w["w_down"])


def adamw(w, m, v, g):
    m = 0.9 * m + 0.1 * g
    v = 0.95 * v + 0.05 * g * g
    step = m * lax.rsqrt(v + 1e-8) + 0.1 * w
    return (w - 0.02 * step).astype(jnp.bfloat16), m, v


class Place:
    def __init__(self, side):
        self.side = side
        me = lax.axis_index("dp")
        self.c = lax.rem(me, CORES)
        self.y = lax.rem(me // CORES, side)
        self.x = me // (CORES * side)

    def device(self, x, y, c):
        return {"dp": (x * self.side + y) * CORES + c}

    def partner(self):
        return self.device(self.x, self.y, 1 - self.c)

    def along(self, axis, k):
        if axis == "x":
            x = lax.rem(self.x + k, self.side)
            return x, self.device(x, self.y, self.c)
        y = lax.rem(self.y + k, self.side)
        return y, self.device(self.x, y, self.c)

    def barrier(self):
        sem = pltpu.get_barrier_semaphore()
        others = [self.partner()] + [self.along(a, k)[1] for a in "xy" for k in range(1, self.side)]
        for other in others:
            pl.semaphore_signal(sem, inc=1, device_id=other, device_id_type=MESH)
        pl.semaphore_wait(sem, len(others))


def send(src, dst, sems, device):
    return pltpu.make_async_remote_copy(
        src_ref=src, dst_ref=dst, send_sem=sems[0], recv_sem=sems[1], device_id=device, device_id_type=MESH
    )


class Gather:
    def __init__(self, place, whole, send_sems, recv_sems, first):
        p, s = place, place.side
        sems = [(send_sems.at[i], recv_sems.at[i]) for i in range(2 * s - 1)]
        second = "y" if first == "x" else "x"
        own = whole.at[p.x, p.y, p.c]
        line = whole.at[:, p.y, p.c] if first == "x" else whole.at[p.x, :, p.c]
        plane = whole.at[:, :, p.c]
        self.stages = [
            [send(own, own, sems[k - 1], p.along(first, k)[1]) for k in range(1, s)],
            [send(line, line, sems[s - 2 + k], p.along(second, k)[1]) for k in range(1, s)],
            [send(plane, plane, sems[2 * s - 2], p.partner())],
        ]

    def start(self, stage):
        for copy in self.stages[stage]:
            copy.start()

    def wait(self, stage):
        for copy in self.stages[stage]:
            copy.wait()


def gather_kernel(side, *refs):
    shards, wholes, (send_sems, recv_sems, local_sems) = refs[:3], refs[3:9], refs[9:]
    p = Place(side)
    units = []
    for i, whole in enumerate(wholes):
        number, which = divmod(i, 3)
        pltpu.make_async_copy(shards[which].at[number], whole.at[p.x, p.y, p.c], local_sems.at[i]).start()
        units.append(Gather(p, whole, send_sems.at[i], recv_sems.at[i], "xy"[i % 2]))
    p.barrier()
    for i, whole in enumerate(wholes):
        number, which = divmod(i, 3)
        pltpu.make_async_copy(shards[which].at[number], whole.at[p.x, p.y, p.c], local_sems.at[i]).wait()
        units[i].start(0)
    for stage in range(3):
        for unit in units:
            unit.wait(stage)
            if stage < 2:
                unit.start(stage + 1)


def gathered(side, weights):
    layers = weights[0].shape[0]
    wholes = [jax.ShapeDtypeStruct((side, side, CORES) + w.shape[1:], w.dtype) for _ in range(layers) for w in weights]
    count = len(wholes)
    out = pl.pallas_call(
        functools.partial(gather_kernel, side),
        out_shape=wholes,
        in_specs=[HBM] * 3,
        out_specs=[HBM] * count,
        scratch_shapes=[
            pltpu.SemaphoreType.DMA((count, 2 * side - 1)),
            pltpu.SemaphoreType.DMA((count, 2 * side - 1)),
            pltpu.SemaphoreType.DMA((count,)),
        ],
        compiler_params=pltpu.CompilerParams(collective_id=0, has_side_effects=True),
        name="gather",
    )(*weights)
    return [w.reshape(-1, w.shape[-1]) for w in out]


class Scatter:
    def __init__(self, place, refs, send_sems, recv_sems, first):
        p, s = place, place.side
        self.p, self.s, self.first, self.refs = p, s, first, refs
        mine, pair, paired, line, lined, last, _ = refs
        sems = [(send_sems.at[i], recv_sems.at[i]) for i in range(2 * s - 1)]
        second = "y" if first == "x" else "x"
        self.stages = [[send(mine.at[:, :, 1 - p.c], pair, sems[0], p.partner())], [], []]
        for k in range(1, s):
            there, device = p.along(first, k)
            part = paired.at[there] if first == "x" else paired.at[:, there]
            self.stages[1].append(send(part, line.at[k - 1], sems[k], device))
        for k in range(1, s):
            there, device = p.along(second, k)
            self.stages[2].append(send(lined.at[there], last.at[k - 1], sems[s - 1 + k], device))

    def start(self, stage):
        for copy in self.stages[stage]:
            copy.start()

    def wait(self, stage):
        for copy in self.stages[stage]:
            copy.wait()

    def _pair_sum(self, x, y):
        mine, pair = self.refs[:2]
        return mine[x, y, self.p.c].astype(jnp.float32) + pair[x, y].astype(jnp.float32)

    def _line_sum(self, i):
        p, line = self.p, self.refs[3]
        total = self._pair_sum(p.x, i) if self.first == "x" else self._pair_sum(i, p.y)
        for k in range(self.s - 1):
            total += line[k, i].astype(jnp.float32)
        return total

    def add(self, stage):
        p, s = self.p, self.s
        mine, pair, paired, line, lined, last, out = self.refs
        if stage == 0:

            @pl.loop(0, s * s)
            def _(i):
                x, y = i // s, lax.rem(i, s)
                paired[x, y] = self._pair_sum(x, y).astype(paired.dtype)

        elif stage == 1:

            @pl.loop(0, s)
            def _(i):
                lined[i] = self._line_sum(i).astype(lined.dtype)

        else:
            total = self._line_sum(p.y if self.first == "x" else p.x)
            for k in range(s - 1):
                total += last[k].astype(jnp.float32)
            total = total.astype(out.dtype)
            out[...] = total
            return total


def scatter_kernel(side, count, *refs):
    grads, outs, norm = refs[:count], refs[count : 2 * count], refs[2 * count]
    rest = refs[2 * count + 1 :]
    tables = [rest[i * count : (i + 1) * count] for i in range(5)]
    squares, others, send_sems, recv_sems, norm_send, norm_recv = rest[5 * count :]
    p = Place(side)
    units = [
        Scatter(p, (grads[i], *(t[i] for t in tables), outs[i]), send_sems.at[i], recv_sems.at[i], "xy"[i % 2]) for i in range(count)
    ]
    p.barrier()
    for unit in units:
        unit.start(0)
    total = jnp.zeros((8, 128), jnp.float32)
    for stage in range(3):
        for unit in units:
            unit.wait(stage)
            g = unit.add(stage)
            if stage < 2:
                unit.start(stage + 1)
            else:
                wide = g.astype(jnp.float32)
                wide = wide * wide
                total += wide.reshape(-1, 8, 128).sum(0) if wide.shape[-1] == 128 else fold(wide)
    norm[...] = reduced(p, total, squares, others, norm_send, norm_recv)


def fold(wide):
    rows, columns = wide.shape
    rows8 = wide.reshape(rows // 8, 8, columns).sum(0)
    total = rows8[:, :128]
    for i in range(128, columns, 128):
        total += rows8[:, i : i + 128]
    return total


def reduced(p, total, squares, others, send_sems, recv_sems):
    at = 0
    for stage, devices in enumerate(
        ([p.partner()], [p.along("y", k)[1] for k in range(1, p.side)], [p.along("x", k)[1] for k in range(1, p.side)])
    ):
        squares[stage] = total
        copies = []
        for device in devices:
            copies.append(send(squares.at[stage], others.at[at], (send_sems.at[at], recv_sems.at[at]), device))
            at += 1
        for copy in copies:
            copy.start()
        for copy in copies:
            copy.wait()
        for i in range(at - len(copies), at):
            total = total + others[i]
    return total


def scattered(side, grads):
    count = len(grads)
    owners = (side, side, CORES)
    blocks = [(g.shape[0] // math.prod(owners), g.shape[1]) for g in grads]
    shaped = [g.reshape(owners + b) for g, b in zip(grads, blocks)]
    leads = [(side, side), (side, side), (side - 1, side), (side,), (side - 1,)]
    stages = 2 * side - 1
    out = pl.pallas_call(
        functools.partial(scatter_kernel, side, count),
        out_shape=[jax.ShapeDtypeStruct(b, jnp.bfloat16) for b in blocks] + [jax.ShapeDtypeStruct((8, 128), jnp.float32)],
        in_specs=[VMEM] * count,
        out_specs=[VMEM] * (count + 1),
        scratch_shapes=[pltpu.VMEM(lead + b, jnp.bfloat16) for lead in leads for b in blocks]
        + [
            pltpu.VMEM((3, 8, 128), jnp.float32),
            pltpu.VMEM((stages, 8, 128), jnp.float32),
            pltpu.SemaphoreType.DMA((count, stages)),
            pltpu.SemaphoreType.DMA((count, stages)),
            pltpu.SemaphoreType.DMA((stages,)),
            pltpu.SemaphoreType.DMA((stages,)),
        ],
        compiler_params=pltpu.CompilerParams(collective_id=1, has_side_effects=True, vmem_limit_bytes=60 << 20),
        name="scatter",
    )(*shaped)
    return out[:count], out[count]


def solution(mesh):
    side = math.isqrt(mesh.shape["dp"] // CORES)

    def step(x, dy, *arrays):
        weights, m, v = (arrays[i : i + 3] for i in (0, 3, 6))
        layers = weights[0].shape[0]
        whole = gathered(side, weights)
        fetched = [dict(zip(NAMES, whole[3 * n : 3 * n + 3], strict=True)) for n in range(layers)]
        h, kept = x[0], []
        for number in range(layers):
            kept.append(h)
            h = layer(h, fetched[number])
        by_h, grads = dy[0], []
        for number in reversed(range(layers)):
            _, back = jax.vjp(lambda w, h: layer(h, w), fetched[number], kept[number])
            by_w, by_h = back(by_h)
            grads = [by_w[name] for name in NAMES] + grads
        mine, squares = scattered(side, grads)
        gradients = [jnp.stack([mine[3 * n + i] for n in range(layers)]).astype(jnp.float32) for i in range(3)]
        count = mesh.shape["dp"] * sum(g.size for g in gradients)
        factor = jnp.minimum(1.0, 0.5 * lax.rsqrt(jnp.sum(squares) / count + 1e-30))
        new = [adamw(w.astype(jnp.float32), m, v, g * factor) for w, m, v, g in zip(weights, m, v, gradients, strict=True)]
        return tuple(one[which] for which in range(3) for one in new)

    states, cut = P(("rep", "dp"), None, None), P(None, "dp", None)
    return jax.shard_map(
        step,
        mesh=mesh,
        in_specs=(states, states) + (cut,) * 9,
        out_specs=(P("rep", "dp", None),) * 9,
        check_vma=False,
    )
```

time: 857 us -> 456 us (0.53)
  waiting for transfers between devices: 507 us -> 0 us
  Pallas kernels: 0 us -> 176 us
  blocking collectives: 46.2 us -> 0 us
  between operations: 17.5 us -> 2.03 us
    reduce_scatter x6 -> x0, waiting for transfers between devices: 340 us -> none  [step(): lax.psum_scatter(by_w[name], 'dp', scatter_dimension=0, tiled=True)]
    pallas_call x0 -> x2, Pallas kernels: none -> 176 us  [the longest x1 89.9 us: scattered(): pl.pallas_call(functools.partial(scatter_kernel, side, count), out_shape=...]
    all_gather x6 -> x0, waiting for transfers between devices: 166 us -> none  [fetched(): lax.all_gather(w[number], 'dp', axis=0, tiled=True)]
    psum x1 -> x0, blocking collectives: 46.2 us -> none  [step(): squares = lax.psum(sum((jnp.sum(g * g) for g in gradients)), 'dp')]
  transfers between devices with their start and end apart: 12 -> 0, of which waited for: 11 -> 0; matrix products, arithmetic and copies ran while one was open for 23% -> 0% of each run, Pallas kernels for 0% -> 0%
where the time goes in v1:
time: 456 us; the launch traced here: 448 us
  matrix products  254 us (56%)
  Pallas kernels  176 us (39%)
  other arithmetic  9.81 us (2%)
  local copies, waits for them, and re-layouts  5.97 us (1%)
    dot_general x5, matrix products, layer(): gate = jnp.dot(a, w['w_gate'], preferred_element_type=jnp.float32)  99.6 us
    dot_general x5, matrix products, layer(): up = jnp.dot(a, w['w_up'], preferred_element_type=jnp.float32)  92.3 us
    pallas_call x1, Pallas kernels, scattered(): pl.pallas_call(functools.partial(scatter_kernel, side, count), out_shape=...  89.9 us
    pallas_call x1, Pallas kernels, gathered(): pl.pallas_call(functools.partial(gather_kernel, side), out_shape=wholes,...  86.5 us
    dot_general x5, matrix products, matmul(): jnp.dot(a, w, preferred_element_type=jnp.float32).astype(jnp.bfloat16)  61.7 us

profile of v1, /device:TPU:97, one launch (start us, length us, event | category | flops | bytes accessed | tf_op | source)
XLA Modules:
  0.0 447.9 jit_solution(11534551064520193827)
XLA Ops:
  0.6 2.9 copy.20
  3.6 0.5 fusion.22
  4.1 0.0 copy-start.17
  4.1 86.5 %gather.1 = (bf16[4,4,2,16,3072]{4,3,2,1,0:T(8,128)(2,1)}, bf16[4,4,2,16,3072]{4,3,2,1,0:T(8,128)(2,1)}, bf16[4,4,2,96,512]{4,3,2,1,0:T(8,128)(2,1)}, bf16[4,4,2...) custom-call(bf16[2,16,3072]{2,1,0:T(8,128)(2,1)} %refs_0_.1, ...), custom_call_target="tpu_custom_call" | custom-call | tf_op jit(solution)/shard_map/gather/pallas_call | solution.py:124
  90.6 0.0 copy-start.2
  90.6 14.1 %fusion.46 = f32[2048,3072]{1,0:T(8,128)} fusion(bf16[512,3072]{1,0:T(8,128)(2,1)} %bitcast.84, bf16[1,2048,512]{2,1,0:T(8,128)(2,1)} %param.11, f32[2048]{0:T(1024)S(1)} %add_rsqrt_fusion), kind=kOutput, calls=%fused_computation.59 | convolution fusion | flops 6445596672 | bytes 30416896 | tf_op jit(solution)/shard_map/dot_general | solution.py:30
  104.7 23.5 %multiply_convert_fusion.1 = (bf16[2048,3072]{1,0:T(8,128)(2,1)}, f32[2048,3072]{1,0:T(8,128)}) fusion(f32[2048,3072]{1,0:T(8,128)} %fusion.46, bf16[512,3072]{1,0:T(8,128)(2,1)} %bitcast.83, bf16[1,2048,512]{2,1,0:T(8,128)(2,1)S(1)} %copy-done.2, f32[2048]{0:T(1024)S(1)} %add_rsqrt_fusion), kind=kOutput, calls=%fused_computation.17 | convolution fusion | flops 6483345408 | bytes 68165632 | tf_op jit(solution)/shard_map/dot_general | solution.py:31
  128.2 10.8 %fusion.26 = (f32[2048]{0:T(1024)S(1)}, bf16[2048,512]{0,1:T(8,128)(2,1)S(1)}) fusion(bf16[2048,3072]{1,0:T(8,128)(2,1)} %get-tuple-element.44, bf16[3072,512]{1,0:T(8,128)(2,1)} %bitcast.76, bf16[1,2048,512]{1,2,0:T(8,128)(2,1)S(1)} %copy.20), kind=kOutput, calls=%fused_computation.43 | convolution fusion | flops 6447691776 | bytes 19931136 | tf_op jit(solution)/shard_map/dot_general | solution.py:19
  139.0 0.0 copy-start.15
  139.0 0.0 copy-start.3
  139.0 14.8 %fusion.40 = f32[2048,3072]{1,0:T(8,128)} fusion(bf16[512,3072]{1,0:T(8,128)(2,1)} %bitcast.80, bf16[2048,512]{0,1:T(8,128)(2,1)S(1)} %get-tuple-element.47, f32[2048]{0:T(1024)S(1)} %fusion.60), kind=kOutput, calls=%fused_computation.56 | convolution fusion | flops 6445596672 | bytes 30416896 | tf_op jit(solution)/shard_map/jvp()/dot_general | solution.py:31
  153.9 9.6 %convolution_convert_fusion.1 = bf16[3072,2048]{0,1:T(8,128)(2,1)} fusion(bf16[3072,512]{1,0:T(8,128)(2,1)S(1)} %bitcast.82, bf16[1,2048,512]{2,1,0:T(8,128)(2,1)S(1)} %copy-done.3), kind=kOutput, calls=%fused_computation.25 | convolution fusion | flops 6448742400 | bytes 17825792 | tf_op jit(solution)/shard_map/transpose(jvp())/dot_general | solution.py:19
  163.5 36.1 %fusion.2 = (bf16[2048,3072]{1,0:T(8,128)(2,1)}, f32[2048,3072]{1,0:T(8,128)}) fusion(f32[2048,3072]{1,0:T(8,128)} %fusion.40, bf16[3072,2048]{0,1:T(8,128)(2,1)} %convolution_convert_fusion.1, bf16[512,3072]{1,0:T(8,128)(2,1)} %bitcast.78, bf16[2048,512]{0,1:T(8,128)(2,1)} %copy-done.4, f32[2048]{0:T(1024)S(1)} %fusion.60), kind=kOutput, calls=%fused_computation.6 | convolution fusion | flops 6521094144 | bytes 80748544 | tf_op jit(solution)/shard_map/jvp()/dot_general | solution.py:30
  199.6 20.1 %fusion.15 = bf16[3072,512]{1,0:T(8,128)(2,1)} fusion(f32[2048,3072]{1,0:T(8,128)} %fusion.40, bf16[1,2048,512]{2,1,0:T(8,128)(2,1)S(1)} %copy-done.3, f32[2048,3072]{1,0:T(8,128)} %get-tuple-element.49), kind=kOutput, calls=%fused_computation.33 | convolution fusion | flops 6481772544 | bytes 55574528 | tf_op jit(solution)/shard_map/transpose(jvp())/dot_general | solution.py:19
  219.7 18.4 %fusion.16 = bf16[512,3072]{1,0:T(8,128)(2,1)} fusion(bf16[3072,2048]{0,1:T(8,128)(2,1)} %convolution_convert_fusion.1, bf16[2048,512]{0,1:T(8,128)(2,1)} %copy-done.4, f32[2048]{0:T(1024)S(1)} %fusion.60, f32[2048,3072]{1,0:T(8,128)} %get-tuple-element.49), kind=kOutput, calls=%fused_computation.34 | convolution fusion | flops 6484918272 | bytes 42999808 | tf_op jit(solution)/shard_map/transpose(jvp())/dot_general | solution.py:31
  238.1 10.8 %convolution_convert_fusion.2 = bf16[512,3072]{1,0:T(8,128)(2,1)} fusion(bf16[2048,3072]{1,0:T(8,128)(2,1)} %get-tuple-element.48, bf16[2048,512]{0,1:T(8,128)(2,1)S(1)} %copy-done.5, f32[2048]{0:T(1024)S(1)} %fusion.60), kind=kOutput, calls=%fused_computation.36 | convolution fusion | flops 6445596672 | bytes 17833984 | tf_op jit(solution)/shard_map/transpose(jvp())/dot_general | solution.py:30
  248.9 18.1 %fusion.29 = bf16[2048,512]{0,1:T(8,128)(2,1)} fusion(bf16[512,3072]{1,0:T(8,128)(2,1)} %bitcast.81, bf16[3072,2048]{0,1:T(8,128)(2,1)} %convolution_convert_fusion.1, f32[2048,3072]{1,0:T(8,128)} %get-tuple-element.49), kind=kOutput, calls=%fused_computation.47 | convolution fusion | flops 6481248256 | bytes 42991616 | tf_op jit(solution)/shard_map/transpose(jvp())/dot_general | solution.py:31
  267.0 13.7 %fusion.28 = (f32[2048]{0:T(1024)S(1)}, bf16[2048,512]{0,1:T(8,128)(2,1)}) fusion(bf16[2048,512]{0,1:T(8,128)(2,1)S(1)} %copy-done.5, bf16[2048,512]{0,1:T(8,128)(2,1)} %fusion.29, bf16[2048,3072]{1,0:T(8,128)(2,1)} %get-tuple-element.48, bf16[512,3072]{1,0:T(8,128)(2,1)} %bitcast.79), kind=kOutput, calls=%fused_computation.45 | convolution fusion | flops 6447691776 | bytes 22028288 | tf_op jit(solution)/shard_map/transpose(jvp())/dot_general | solution.py:30
  280.7 2.9 copy.21
  283.6 3.6 fusion.33
  287.2 11.4 %convolution_convert_fusion.3 = bf16[3072,512]{1,0:T(8,128)(2,1)} fusion(bf16[2048,3072]{1,0:T(8,128)(2,1)} %get-tuple-element.44, bf16[2048,512]{0,1:T(8,128)(2,1)S(1)} %fusion.33), kind=kOutput, calls=%fused_computation.37 | convolution fusion | flops 6444023808 | bytes 17825792 | tf_op jit(solution)/shard_map/transpose(jvp())/dot_general | solution.py:19
  298.6 9.8 %convolution_convert_fusion = bf16[2048,3072]{1,0:T(8,128)(2,1)} fusion(bf16[2048,512]{0,1:T(8,128)(2,1)S(1)} %fusion.33, bf16[3072,512]{1,0:T(8,128)(2,1)S(1)} %bitcast.77), kind=kOutput, calls=%fused_computation.24 | convolution fusion | flops 6448742400 | bytes 17825792 | tf_op jit(solution)/shard_map/transpose(jvp())/dot_general | solution.py:19
  308.4 17.5 %fusion.17 = bf16[512,3072]{1,0:T(8,128)(2,1)} fusion(bf16[2048,3072]{1,0:T(8,128)(2,1)} %convolution_convert_fusion, f32[2048,3072]{1,0:T(8,128)} %fusion.46, bf16[1,2048,512]{1,2,0:T(8,128)(2,1)S(1)} %copy-done.1, f32[2048]{0:T(1024)S(1)} %copy-done.18), kind=kOutput, calls=%fused_computation.35 | convolution fusion | flops 6484918272 | bytes 42999808 | tf_op jit(solution)/shard_map/transpose(jvp())/dot_general | solution.py:31
  325.9 25.0 %fusion.18 = bf16[512,3072]{1,0:T(8,128)(2,1)} fusion(f32[2048,3072]{1,0:T(8,128)} %fusion.46, f32[2048,3072]{1,0:T(8,128)} %get-tuple-element.45, bf16[2048,3072]{1,0:T(8,128)(2,1)} %convolution_convert_fusion, bf16[1,2048,512]{1,2,0:T(8,128)(2,1)S(1)} %copy-done.1, f32[2048]{0:T(1024)S(1)} %copy-done.18), kind=kOutput, calls=%fused_computation.38 | convolution fusion | flops 6516375552 | bytes 68165632 | tf_op jit(solution)/shard_map/transpose(jvp())/dot_general | solution.py:30
  350.9 0.0 copy-start.7
  350.9 0.0 copy-start.11
  350.9 0.0 copy-start.13
  351.0 0.0 copy-start.14
  351.0 89.9 %scatter.1 = (bf16[16,3072]{1,0:T(8,128)(2,1)}, bf16[16,3072]{1,0:T(8,128)(2,1)}, bf16[96,512]{1,0:T(8,128)(2,1)}, bf16[16,3072]{1,0:T(8,128)(2,1)}, bf16[16,307...) custom-call(bf16[4,4,2,16,3072]{4,3,2,1,0:T(8,128)(2,1)} %bitcast.69, ...), custom_call_target="tpu_custom_call" | custom-call | tf_op jit(solution)/shard_map/scatter/pallas_call | solution.py:261
  440.9 1.3 reduce_sum.41
  442.9 2.0 fusion.56
  444.9 2.5 fusion.50
  (37 shorter events, 0.1 us)
Async XLA Ops:
  3.6 124.6 %copy-start = (bf16[1,2048,512]{1,2,0:T(8,128)(2,1)}, bf16[1,2048,512]{1,2,0:T(8,128)(2,1)S(1)}, u32[]{:S(2)}) copy-start(bf16[1,2048,512]{1,2,0:T(8,128)(2,1)S(1)} %copy.20) | copy-start | bytes 6291460
  4.1 100.6 %copy-start.17 = (f32[2048]{0:T(1024)}, f32[2048]{0:T(1024)S(1)}, u32[]{:S(2)}) copy-start(f32[2048]{0:T(1024)S(1)} %add_rsqrt_fusion) | copy-start | bytes 24580
  90.6 14.1 %copy-start.2 = (bf16[1,2048,512]{2,1,0:T(8,128)(2,1)S(1)}, bf16[1,2048,512]{2,1,0:T(8,128)(2,1)}, u32[]{:S(2)}) copy-start(bf16[1,2048,512]{2,1,0:T(8,128)(2,1)} %param.11) | copy-start | bytes 6291460
  139.0 14.8 %copy-start.4 = (bf16[2048,512]{0,1:T(8,128)(2,1)}, bf16[2048,512]{0,1:T(8,128)(2,1)S(1)}, u32[]{:S(2)}) copy-start(bf16[2048,512]{0,1:T(8,128)(2,1)S(1)} %get-tuple-element.47) | copy-start | bytes 6291460
  139.0 14.8 %copy-start.15 = (f32[2048]{0:T(1024)}, f32[2048]{0:T(1024)S(1)}, u32[]{:S(2)}) copy-start(f32[2048]{0:T(1024)S(1)} %get-tuple-element.46) | copy-start | bytes 24580
  139.0 14.8 %copy-start.3 = (bf16[1,2048,512]{2,1,0:T(8,128)(2,1)S(1)}, bf16[1,2048,512]{2,1,0:T(8,128)(2,1)}, u32[]{:S(2)}) copy-start(bf16[1,2048,512]{2,1,0:T(8,128)(2,1)} %param.12) | copy-start | bytes 6291460
  139.0 14.8 %copy-start.20 = (bf16[4,4,2,96,512]{4,3,2,1,0:T(8,128)(2,1)S(1)}, bf16[4,4,2,96,512]{4,3,2,1,0:T(8,128)(2,1)}, u32[]{:S(2)}) copy-start(bf16[4,4,2,96,512]{4,3,2,1,0:T(8,128)(2,1)} %get-tuple-element.26) | copy-start | bytes 9437188
  219.7 18.4 %copy-start.5 = (bf16[2048,512]{0,1:T(8,128)(2,1)S(1)}, bf16[2048,512]{0,1:T(8,128)(2,1)}, u32[]{:S(2)}) copy-start(bf16[2048,512]{0,1:T(8,128)(2,1)} %copy-done.4) | copy-start | bytes 6291460
  267.0 13.7 %copy-start.16 = (f32[2048]{0:T(1024)S(1)}, f32[2048]{0:T(1024)}, u32[]{:S(2)}) copy-start(f32[2048]{0:T(1024)} %copy-done.15) | copy-start | bytes 24580
  287.2 11.4 %copy-start.19 = (bf16[4,4,2,96,512]{4,3,2,1,0:T(8,128)(2,1)S(1)}, bf16[4,4,2,96,512]{4,3,2,1,0:T(8,128)(2,1)}, u32[]{:S(2)}) copy-start(bf16[4,4,2,96,512]{4,3,2,1,0:T(8,128)(2,1)} %get-tuple-element.24) | copy-start | bytes 9437188
  298.6 9.8 %copy-start.1 = (bf16[1,2048,512]{1,2,0:T(8,128)(2,1)S(1)}, bf16[1,2048,512]{1,2,0:T(8,128)(2,1)}, u32[]{:S(2)}) copy-start(bf16[1,2048,512]{1,2,0:T(8,128)(2,1)} %copy-done) | copy-start | bytes 6291460
  298.6 9.8 %copy-start.18 = (f32[2048]{0:T(1024)S(1)}, f32[2048]{0:T(1024)}, u32[]{:S(2)}) copy-start(f32[2048]{0:T(1024)} %copy-done.17) | copy-start | bytes 24580
  350.9 92.0 %copy-start.8 = (bf16[2,96,512]{2,1,0:T(8,128)(2,1)S(1)}, bf16[2,96,512]{2,1,0:T(8,128)(2,1)}, u32[]{:S(2)}) copy-start(bf16[2,96,512]{2,1,0:T(8,128)(2,1)} %refs_2_.1) | copy-start | bytes 589828
  350.9 92.0 %copy-start.9 = (f32[2,96,512]{2,1,0:T(8,128)S(1)}, f32[2,96,512]{2,1,0:T(8,128)}, u32[]{:S(2)}) copy-start(f32[2,96,512]{2,1,0:T(8,128)} %param.21) | copy-start | bytes 1179652
  350.9 92.0 %copy-start.10 = (f32[2,96,512]{2,1,0:T(8,128)S(1)}, f32[2,96,512]{2,1,0:T(8,128)}, u32[]{:S(2)}) copy-start(f32[2,96,512]{2,1,0:T(8,128)} %param.18) | copy-start | bytes 1179652
  350.9 94.0 %copy-start.6 = (bf16[2,16,3072]{2,1,0:T(8,128)(2,1)S(1)}, bf16[2,16,3072]{2,1,0:T(8,128)(2,1)}, u32[]{:S(2)}) copy-start(bf16[2,16,3072]{2,1,0:T(8,128)(2,1)} %refs_0_.1) | copy-start | bytes 589828
  350.9 94.0 %copy-start.7 = (bf16[2,16,3072]{2,1,0:T(8,128)(2,1)S(1)}, bf16[2,16,3072]{2,1,0:T(8,128)(2,1)}, u32[]{:S(2)}) copy-start(bf16[2,16,3072]{2,1,0:T(8,128)(2,1)} %refs_1_.1) | copy-start | bytes 589828
  350.9 94.0 %copy-start.11 = (f32[2,16,3072]{2,1,0:T(8,128)S(1)}, f32[2,16,3072]{2,1,0:T(8,128)}, u32[]{:S(2)}) copy-start(f32[2,16,3072]{2,1,0:T(8,128)} %param.19) | copy-start | bytes 1179652
  350.9 94.0 %copy-start.12 = (f32[2,16,3072]{2,1,0:T(8,128)S(1)}, f32[2,16,3072]{2,1,0:T(8,128)}, u32[]{:S(2)}) copy-start(f32[2,16,3072]{2,1,0:T(8,128)} %param.16) | copy-start | bytes 1179652
  350.9 94.0 %copy-start.13 = (f32[2,16,3072]{2,1,0:T(8,128)S(1)}, f32[2,16,3072]{2,1,0:T(8,128)}, u32[]{:S(2)}) copy-start(f32[2,16,3072]{2,1,0:T(8,128)} %param.20) | copy-start | bytes 1179652
  351.0 94.0 %copy-start.14 = (f32[2,16,3072]{2,1,0:T(8,128)S(1)}, f32[2,16,3072]{2,1,0:T(8,128)}, u32[]{:S(2)}) copy-start(f32[2,16,3072]{2,1,0:T(8,128)} %param.17) | copy-start | bytes 1179652

commit v2 on v0

v2 whole, which is shorter than its diff:
```python
import functools
import math

import jax
import jax.numpy as jnp
from jax import lax
from jax.experimental import pallas as pl
from jax.experimental.pallas import tpu as pltpu
from jax.sharding import PartitionSpec as P

MESH = pl.DeviceIdType.MESH
CORES = 2
WIDE = 256
BLOCKS = 3
CHUNK = WIDE * BLOCKS
ROWS = 256
VMEM = pl.BlockSpec(memory_space=pltpu.VMEM)
HBM = pl.BlockSpec(memory_space=pl.ANY)
BF16, F32 = jnp.bfloat16, jnp.float32


def dot(a, b):
    return jnp.dot(a, b, preferred_element_type=F32)


def dot_t(a, b):
    return lax.dot_general(a, b, (((1,), (1,)), ((), ())), preferred_element_type=F32)


def adamw(w, m, v, g):
    m = 0.9 * m + 0.1 * g
    v = 0.95 * v + 0.05 * g * g
    step = m * lax.rsqrt(v + 1e-8) + 0.1 * w
    return (w - 0.02 * step).astype(BF16), m, v


class Place:
    def __init__(self, side):
        self.side = side
        me = lax.axis_index("dp")
        self.c = lax.rem(me, CORES)
        self.y = lax.rem(me // CORES, side)
        self.x = me // (CORES * side)

    def device(self, x, y, c):
        return {"dp": (x * self.side + y) * CORES + c}

    def partner(self):
        return self.device(self.x, self.y, 1 - self.c)

    def along(self, axis, k):
        if axis == "x":
            x = lax.rem(self.x + k + self.side, self.side)
            return x, self.device(x, self.y, self.c)
        y = lax.rem(self.y + k + self.side, self.side)
        return y, self.device(self.x, y, self.c)

    def others(self):
        return [self.partner()] + [self.along(a, k)[1] for a in "xy" for k in range(1, self.side)]

    def barrier(self):
        sem = pltpu.get_barrier_semaphore()
        for other in self.others():
            pl.semaphore_signal(sem, inc=1, device_id=other, device_id_type=MESH)
        pl.semaphore_wait(sem, len(self.others()))


def send(src, dst, sems, device):
    return pltpu.make_async_remote_copy(
        src_ref=src, dst_ref=dst, send_sem=sems[0], recv_sem=sems[1], device_id=device, device_id_type=MESH
    )


class Gather:
    STAGES = 5

    def __init__(self, place, whole, rows, cols, send_sems, recv_sems, first):
        p = place
        sems = [(send_sems.at[i], recv_sems.at[i]) for i in range(9)]
        second = "y" if first == "x" else "x"
        half = cols.size // 2
        halves = [pl.ds(cols.start, half), pl.ds(cols.start + half, half)]

        def block(i, cols):
            return whole.at[i, p.y, p.c, rows, cols] if first == "x" else whole.at[p.x, i, p.c, rows, cols]

        def line(i, cols):
            return whole.at[:, i, p.c, rows, cols] if first == "x" else whole.at[i, :, p.c, rows, cols]

        self.stages = []
        for axis, part, base in ((first, block, 0), (second, line, 4)):
            me = p.along(axis, 0)[0]
            (after, up), (before, down) = p.along(axis, 1), p.along(axis, -1)
            mine = part(me, cols)
            self.stages.append([(mine, sems[base], up), (mine, sems[base + 1], down)])
            self.stages.append([(part(before, halves[0]), sems[base + 2], up), (part(after, halves[1]), sems[base + 3], down)])
        self.stages.append([(whole.at[:, :, p.c, rows, cols], sems[8], p.partner())])

    def start(self, stage):
        for part, sems, device in self.stages[stage]:
            send(part, part, sems, device).start()

    def wait(self, stage):
        for part, sems, device in self.stages[stage]:
            send(part, part, sems, device).wait()


class Scatter:
    def __init__(self, place, refs, send_sems, recv_sems, first):
        p, s = place, place.side
        self.p, self.s, self.first, self.refs = p, s, first, refs
        mine, pair, paired, line, lined, last = refs
        sems = [(send_sems.at[i], recv_sems.at[i]) for i in range(2 * s - 1)]
        second = "y" if first == "x" else "x"
        self.stages = [[(mine.at[:, :, 1 - p.c], pair, sems[0], p.partner())], [], []]
        for k in range(1, s):
            there, device = p.along(first, k)
            part = paired.at[there] if first == "x" else paired.at[:, there]
            self.stages[1].append((part, line.at[k - 1], sems[k], device))
        for k in range(1, s):
            there, device = p.along(second, k)
            self.stages[2].append((lined.at[there], last.at[k - 1], sems[s - 1 + k], device))

    def start(self, stage):
        for copy in self.stages[stage]:
            send(*copy).start()

    def wait(self, stage):
        for copy in self.stages[stage]:
            send(*copy).wait()

    def _pair_sum(self, x, y):
        mine, pair = self.refs[:2]
        return mine[x, y, self.p.c].astype(F32) + pair[x, y].astype(F32)

    def _line_sum(self, i):
        p, line = self.p, self.refs[3]
        total = self._pair_sum(p.x, i) if self.first == "x" else self._pair_sum(i, p.y)
        for k in range(self.s - 1):
            total += line[k, i].astype(F32)
        return total

    def add(self, stage):
        s = self.s
        _, _, paired, _, lined, _ = self.refs
        if stage == 0:

            @pl.loop(0, s * s)
            def _(i):
                x, y = i // s, lax.rem(i, s)
                paired[x, y] = self._pair_sum(x, y).astype(BF16)

        else:

            @pl.loop(0, s)
            def _(i):
                lined[i] = self._line_sum(i).astype(BF16)

    def result(self, write):
        p, last = self.p, self.refs[5]
        total = self._line_sum(p.y if self.first == "x" else p.x)
        for k in range(self.s - 1):
            total += last[k].astype(F32)
        write(total.astype(BF16))


class ScatterRows:
    def __init__(self, place, refs, send_sems, recv_sems, owner):
        p, s = place, place.side
        self.p, self.s, self.refs, self.owner = p, s, refs, owner
        mine, pair, paired, line, lined, last = refs
        sems = [(send_sems.at[i], recv_sems.at[i]) for i in range(2 * s - 1)]
        self.first = [(mine.at[:, 1 - p.c], pair, sems[0], p.partner())]
        self.second = []
        for k in range(1, s):
            there, device = p.along("y", k)
            self.second.append((paired.at[there], line.at[k - 1], sems[k], device))
        self.last_sems = [sems[s - 1 + k] for k in range(1, s)]
        self.away = lax.rem(owner - p.x + s, s)

    def _last(self, k):
        lined, last = self.refs[4:]
        return send(lined, last.at[k - 1], self.last_sems[k - 1], self.p.device(self.owner, self.p.y, self.p.c))

    def start(self, stage):
        if stage < 2:
            for copy in (self.first, self.second)[stage]:
                send(*copy).start()
        else:
            for k in range(1, self.s):

                @pl.when(self.away == k)
                def _():
                    self._last(k).start()

    def wait(self, stage):
        if stage < 2:
            for copy in (self.first, self.second)[stage]:
                send(*copy).wait()
        else:
            for k in range(1, self.s):

                @pl.when(self.away == k)
                def _():
                    self._last(k).wait_send()

                @pl.when(self.away == 0)
                def _():
                    self._last(k).wait_recv()

    def _pair_sum(self, y):
        mine, pair = self.refs[:2]
        return mine[y, self.p.c].astype(F32) + pair[y].astype(F32)

    def _line_sum(self):
        total = self._pair_sum(self.p.y)
        for k in range(self.s - 1):
            total += self.refs[3][k].astype(F32)
        return total

    def add(self, stage):
        _, _, paired, _, lined, _ = self.refs
        if stage == 0:

            @pl.loop(0, self.s)
            def _(y):
                paired[y] = self._pair_sum(y).astype(BF16)

        else:
            lined[...] = self._line_sum().astype(BF16)

    def result(self, write):
        @pl.when(self.away == 0)
        def _():
            total = self._line_sum()
            for k in range(self.s - 1):
                total += self.refs[5][k].astype(F32)
            write(total.astype(BF16))


def fold(wide):
    rows, columns = wide.shape
    rows8 = wide.reshape(rows // 8, 8, columns).sum(0)
    total = rows8[:, :128]
    for i in range(128, columns, 128):
        total += rows8[:, i : i + 128]
    return total


def reduced(p, total, squares, others, send_sems, recv_sems):
    at = 0
    for stage, devices in enumerate(
        ([p.partner()], [p.along("y", k)[1] for k in range(1, p.side)], [p.along("x", k)[1] for k in range(1, p.side)])
    ):
        squares[stage] = total
        copies = []
        for device in devices:
            copies.append(send(squares.at[stage], others.at[at], (send_sems.at[at], recv_sems.at[at]), device))
            at += 1
        for copy in copies:
            copy.start()
        for copy in copies:
            copy.wait()
        for i in range(at - len(copies), at):
            total = total + others[i]
    return total


def rms(wide):
    return lax.rsqrt(jnp.mean(wide * wide, -1, keepdims=True) + 1e-6)


def kernel(side, x_in, dy_in, g_in, u_in, d_in, og, ou, od, norm, *scratch):
    (wg, wu, wd, a, a_t, b, b_t, h, acc, p3, squares, others, gg, gu, gd, pg, pu, pd, sg, su, sd, lg, lu, ld, mg, mu, md, eg, eu, ed) = scratch[:30]
    ag_send, ag_recv, rs_send, rs_recv, local, norm_send, norm_recv, free = scratch[30:]
    p = Place(side)
    layers, depth, hidden = wg.shape[0], a.shape[1], wg.shape[-1]
    tokens = a.shape[0]
    chunks = hidden // CHUNK
    steps = layers * chunks
    flat_g, flat_u = (w.reshape(layers, depth, hidden) for w in (wg, wu))
    flat_d = wd.reshape(layers, hidden, depth)

    def shards():
        for i, (shard, whole) in enumerate(((g_in, wg), (u_in, wu), (d_in, wd))):
            for n in range(layers):
                yield pltpu.make_async_copy(shard.at[n], whole.at[n, p.x, p.y, p.c], local.at[i * layers + n])

    def load(i):
        source, target = ((x_in, h), (dy_in, b))[i]
        return pltpu.make_async_copy(source.at[0], target, local.at[3 * layers + i])

    for copy in shards():
        copy.start()
    for i in range(2):
        load(i).start()

    pairs = []

    def pair(*units):
        made = []
        for whole, rows, cols, first in units:
            at = 2 * len(pairs) + len(made)
            made.append(Gather(p, whole, rows, cols, ag_send.at[at], ag_recv.at[at], first))
        pairs.append(made)

    def chunk_pair(n, j):
        rows, cols = pl.ds(0, g_in.shape[1]), pl.ds(j * CHUNK, CHUNK)
        pair((wg.at[n], rows, cols, "x"), (wu.at[n], rows, cols, "y"))

    def down_pairs(n):
        rows, cols = d_in.shape[1] // 2, depth // 2
        for k in range(2):
            pair(
                (wd.at[n], pl.ds(0, rows), pl.ds(k * cols, cols), "x"),
                (wd.at[n], pl.ds(rows, rows), pl.ds(k * cols, cols), "y"),
            )

    for n in range(layers):
        if n == layers - 1:
            down_pairs(n)
        for j in range(chunks):
            if n < layers - 1 and j == chunks - 1:
                down_pairs(n)
            chunk_pair(n, j)

    def gather_round(r):
        if r < len(pairs):
            for unit in pairs[r]:
                unit.start(0)
        for stage in range(Gather.STAGES):
            i = r - 1 - stage
            if 0 <= i < len(pairs):
                for unit in pairs[i]:
                    unit.wait(stage)
                    if stage + 1 < Gather.STAGES:
                        unit.start(stage + 1)

    def columns(j, n=None):
        if n is None:
            return pl.ds(pl.multiple_of(j * CHUNK, CHUNK), CHUNK)
        return pl.ds(pl.multiple_of(j * CHUNK + n * WIDE, WIDE), WIDE)

    def tiles(size, body):
        @pl.loop(0, tokens // size)
        def _(t):
            body(pl.ds(pl.multiple_of(t * size, size), size))

    def forward(n, j, slot):
        @pl.loop(0, BLOCKS)
        def _(i):
            gate, up = dot(a[...], flat_g[n, :, columns(j, i)]), dot(a[...], flat_u[n, :, columns(j, i)])
            p3[slot, :, columns(0, i)] = (jax.nn.silu(gate) * up).astype(BF16)

    def down(n, parts, more):
        @pl.loop(0, depth // WIDE)
        def _(i):
            cols = columns(0, i)
            y = sum(dot(p3[slot], flat_d[n, pl.ds(j * CHUNK, CHUNK), cols]) for j, slot in parts)
            if more:
                acc[:, cols] = y
            else:
                y = (acc[:, cols] + y).astype(BF16)
                h[:, cols] = h[:, cols] + y

    def norms(transposed):
        def body(rows):
            wide = h[rows, :].astype(F32)
            scaled = (wide * rms(wide)).astype(BF16)
            a[rows, :] = scaled
            if transposed:
                a_t[:, rows] = scaled.T

        tiles(ROWS, body)

    def transpose_b(rows):
        b_t[:, rows] = b[rows, :].T

    def backward(n, j, i):
        gate, up = dot(a[...], flat_g[n, :, columns(j, i)]), dot(a[...], flat_u[n, :, columns(j, i)])
        by_z = dot_t(b[...], flat_d[n, columns(j, i), :]).astype(BF16).astype(F32)
        s = jax.nn.sigmoid(gate)
        silu = gate * s
        cols = columns(0, i)
        p3[0, :, cols] = (silu * up).astype(BF16)
        p3[1, :, cols] = (by_z * up * (s + silu * (1 - s))).astype(BF16)
        p3[2, :, cols] = (by_z * silu).astype(BF16)

    def by_normed(n, j):
        @pl.loop(0, depth // WIDE)
        def _(i):
            rows = columns(0, i)
            acc[:, rows] += dot_t(p3[1], flat_g[n, rows, columns(j)]) + dot_t(p3[2], flat_u[n, rows, columns(j)])

    def by_states(rows):
        wide = h[rows, :].astype(F32)
        scale = rms(wide)
        by = acc[rows, :].astype(BF16).astype(F32)
        along = jnp.sum(by * wide, -1, keepdims=True) * (scale * scale * scale) * (1 / depth)
        new = b[rows, :] + (by * scale - wide * along).astype(BF16)
        b[rows, :] = new
        b_t[:, rows] = new.T

    flat_gg, flat_gu = (r.reshape(CORES, depth, CHUNK) for r in (gg, gu))
    flat_gd = gd.reshape(CORES, CHUNK, depth)

    def scatters(q):
        slot, j = lax.rem(q, 2), lax.rem(q, chunks)
        sems = [(rs_send.at[slot, i], rs_recv.at[slot, i]) for i in range(3)]
        at = lambda *refs: [r.at[slot] for r in refs]
        g = Scatter(p, (*at(gg, pg), sg, *at(lg), mg, *at(eg)), *sems[0], "x")
        u = Scatter(p, (*at(gu, pu), su, *at(lu), mu, *at(eu)), *sems[1], "y")
        d = ScatterRows(p, (*at(gd, pd), sd, *at(ld), md, *at(ed)), *sems[2], j)
        return g, u, d

    def finish(q):
        n, j = layers - 1 - q // chunks, lax.rem(q, chunks)
        g, u, d = scatters(q)

        def keep(out, *where):
            def write(total):
                out[where] = total
                wide = total.astype(F32)
                squares[3] = squares[3] + fold(wide * wide)

            return write

        for unit, write in ((g, keep(og, n, slice(None), columns(j))), (u, keep(ou, n, slice(None), columns(j))), (d, keep(od, n))):
            unit.wait(2)
            unit.result(write)

        @pl.when(q + 2 < steps)
        def _():
            for other in p.others():
                pl.semaphore_signal(free.at[lax.rem(q, 2)], inc=1, device_id=other, device_id_type=MESH)

    p.barrier()
    for copy in shards():
        copy.wait()
    last_rounds = Gather.STAGES - 2
    rounds = len(pairs) + Gather.STAGES
    done = 0
    for r in range(rounds - last_rounds):
        gather_round(r)
        if r == 0:
            load(0).wait()
            norms(False)
        elif r == 1:
            load(1).wait()
            tiles(ROWS, transpose_b)
            squares[3] = jnp.zeros_like(squares[3])
        ready = r - Gather.STAGES
        if 0 <= ready < chunks - 1:
            forward(0, ready, ready)
        elif ready == chunks:
            down(0, [(j, j) for j in range(chunks - 1)], True)
        elif ready == chunks + 1:
            forward(0, chunks - 1, 0)
            down(0, [(chunks - 1, 0)], False)
            norms(True)
            acc[...] = jnp.zeros_like(acc)

    @pl.loop(0, steps + 2)
    def _(q):
        n, j, slot = layers - 1 - q // chunks, lax.rem(q, chunks), lax.rem(q, 2)
        computes = q < steps
        sends = (q > 0) & (q <= steps)

        @pl.when(q == chunks)
        def _():
            tiles(ROWS, by_states)
            load(0).start()
            load(0).wait()
            norms(True)

        @pl.when(computes)
        def _():
            backward(n, j, 0)

        @pl.when(sends)
        def _():
            for unit in scatters(q - 1):
                unit.wait(0)
                unit.add(0)
                unit.start(1)

        @pl.when(q >= 2)
        def _():
            finish(q - 2)

        @pl.when(computes)
        def _():
            @pl.loop(1, BLOCKS)
            def _(i):
                backward(n, j, i)

        for k in range(last_rounds):

            @pl.when(q == k)
            def _():
                gather_round(rounds - last_rounds + k)

        @pl.when(computes & (q < chunks))
        def _():
            by_normed(n, j)

        @pl.when(computes)
        def _():
            g, u, _ = scatters(q)
            flat_gg[slot] = dot(a_t[...], p3[1]).astype(BF16)

            @pl.when(q >= 2)
            def _():
                pl.semaphore_wait(free.at[slot], len(p.others()))

            g.start(0)
            flat_gu[slot] = dot(a_t[...], p3[2]).astype(BF16)
            u.start(0)

        @pl.when(sends)
        def _():
            for unit in scatters(q - 1):
                unit.wait(1)
                unit.add(1)
                unit.start(2)

        @pl.when(computes)
        def _():
            flat_gd[slot] = dot(b_t[...], p3[0]).T.astype(BF16)
            scatters(q)[2].start(0)

    norm[...] = reduced(p, squares[3], squares, others, norm_send, norm_recv)


def gradients_of(side, x, dy, weights):
    w_gate, _, w_down = weights
    layers, rows, hidden = w_gate.shape
    rows_d, depth = w_down.shape[1:]
    tokens = x.shape[1]
    chunk, block, rest = (rows, CHUNK), (rows_d, depth), side - 1

    def whole(w):
        return pltpu.VMEM((layers, side, side, CORES) + w.shape[1:], BF16)

    def buffers(lead, lead_d):
        return [pltpu.VMEM(lead + chunk, BF16)] * 2 + [pltpu.VMEM(lead_d + block, BF16)]

    pairs = layers * (hidden // CHUNK + 2)
    stages = 2 * side - 1
    return pl.pallas_call(
        functools.partial(kernel, side),
        out_shape=[jax.ShapeDtypeStruct(w.shape, BF16) for w in weights] + [jax.ShapeDtypeStruct((8, 128), F32)],
        in_specs=[HBM] * 5,
        out_specs=[VMEM] * 4,
        scratch_shapes=[whole(w) for w in weights]
        + [
            pltpu.VMEM((tokens, depth), BF16),
            pltpu.VMEM((depth, tokens), BF16),
            pltpu.VMEM((tokens, depth), BF16),
            pltpu.VMEM((depth, tokens), BF16),
            pltpu.VMEM((tokens, depth), BF16),
            pltpu.VMEM((tokens, depth), F32),
            pltpu.VMEM((3, tokens, CHUNK), BF16),
            pltpu.VMEM((4, 8, 128), F32),
            pltpu.VMEM((stages, 8, 128), F32),
        ]
        + buffers((2, side, side, CORES), (2, side, CORES))
        + buffers((2, side, side), (2, side))
        + buffers((side, side), (side,))
        + buffers((2, rest, side), (2, rest))
        + buffers((side,), ())
        + buffers((2, rest), (2, rest))
        + [
            pltpu.SemaphoreType.DMA((2 * pairs, 9)),
            pltpu.SemaphoreType.DMA((2 * pairs, 9)),
            pltpu.SemaphoreType.DMA((2, 3, stages)),
            pltpu.SemaphoreType.DMA((2, 3, stages)),
            pltpu.SemaphoreType.DMA((3 * layers + 2,)),
            pltpu.SemaphoreType.DMA((stages,)),
            pltpu.SemaphoreType.DMA((stages,)),
            pltpu.SemaphoreType.REGULAR((2,)),
        ],
        compiler_params=pltpu.CompilerParams(collective_id=0, has_side_effects=True, vmem_limit_bytes=67043328),
        name="gradients",
    )(x, dy, *weights)


def solution(mesh):
    side = math.isqrt(mesh.shape["dp"] // CORES)

    def step(x, dy, *arrays):
        weights, m, v = (arrays[i : i + 3] for i in (0, 3, 6))
        *gradients, squares = gradients_of(side, x, dy, weights)
        count = mesh.shape["dp"] * sum(g.size for g in gradients)
        factor = jnp.minimum(1.0, 0.5 * lax.rsqrt(jnp.sum(squares) / count + 1e-30))
        new = [adamw(w.astype(F32), m, v, g.astype(F32) * factor) for w, m, v, g in zip(weights, m, v, gradients, strict=True)]
        return tuple(one[which] for which in range(3) for one in new)

    states, cut = P(("rep", "dp"), None, None), P(None, "dp", None)
    return jax.shard_map(
        step,
        mesh=mesh,
        in_specs=(states, states) + (cut,) * 9,
        out_specs=(P("rep", "dp", None),) * 9,
        check_vma=False,
    )
```

time: 857 us -> 246 us (0.29); the launches traced: 848 us -> 246 us
  waiting for transfers between devices: 507 us -> 0 us
  matrix products: 251 us -> 0 us
  Pallas kernels: 0 us -> 239 us
  blocking collectives: 46.2 us -> 0 us
  between operations: 17.5 us -> 1.4 us
  local copies, waits for them, and re-layouts: 13.5 us -> 0.02 us
    reduce_scatter x6 -> x0, waiting for transfers between devices: 340 us -> none  [step(): lax.psum_scatter(by_w[name], 'dp', scatter_dimension=0, tiled=True)]
    dot_general x15 -> x0, matrix products: 251 us -> none  [the longest x5 92.8 us: layer(): gate = jnp.dot(a, w['w_gate'], preferred_element_type=jnp.float32)]
    pallas_call x0 -> x1, Pallas kernels: none -> 239 us  [gradients_of(): pl.pallas_call(functools.partial(kernel, side), out_shape=[jax.ShapeDtype...]
    all_gather x6 -> x0, waiting for transfers between devices: 166 us -> none  [fetched(): lax.all_gather(w[number], 'dp', axis=0, tiled=True)]
    psum x1 -> x0, blocking collectives: 46.2 us -> none  [step(): squares = lax.psum(sum((jnp.sum(g * g) for g in gradients)), 'dp')]
  transfers between devices with their start and end apart: 12 -> 0, of which waited for: 11 -> 0; matrix products, arithmetic and copies ran while one was open for 23% -> 0% of each run, Pallas kernels for 0% -> 0%
where the time goes in v2:
time: 246 us
  Pallas kernels  239 us (97%)
  other arithmetic  5.52 us (2%)
    pallas_call x1, Pallas kernels, gradients_of(): pl.pallas_call(functools.partial(kernel, side), out_shape=[jax.ShapeDtype...  239 us

profile of v2, /device:TPU:97, one launch (start us, length us, event | category | flops | bytes accessed | tf_op | source)
XLA Modules:
  0.0 246.3 jit_solution(13793944680273326673)
XLA Ops:
  0.6 239.4 %gradients.1 = (bf16[2,16,3072]{2,1,0:T(8,128)(2,1)}, bf16[2,16,3072]{2,1,0:T(8,128)(2,1)}, bf16[2,96,512]{2,1,0:T(8,128)(2,1)}, f32[8,128]{1,0:T(8,128)}) custom-call(bf16[1,2048,512]{2,1,0:T(8,128)(2,1)} %x_in.1, bf16[1,2048,512]{2,1,0:T(8,128)(2,1)} %dy_in.1, bf16[2,16,3072]{2,1,0:T(8,128)(2,1)} %g_in.1, bf16[2,16,3072]{2,1,0:T(8,128)(2,1)} %u_in.1, ...), custom_call_target="tpu_custom_call" | custom-call | tf_op jit(solution)/shard_map/gradients/pallas_call | solution.py:550
  240.0 1.3 reduce_sum.9
  242.0 0.0 copy-start
  242.0 0.0 copy-start.1
  242.0 0.0 copy-start.2
  242.0 0.0 copy-start.3
  242.0 3.2 %fusion.2 = (bf16[2,16,3072]{2,1,0:T(8,128)(2,1)}, f32[2,16,3072]{2,1,0:T(8,128)}, f32[2,16,3072]{2,1,0:T(8,128)}, bf16[2,16,3072]{2,1,0:T(8,128)(2,1)}, f32[2,16,3072]{2,1,0:T(8,128)}, /*index=5*/f32[2,16,3072]{2,1,0:T(8,128)}) fusion(bf16[2,16,3072]{2,1,0:T(8,128)(2,1)} %g_in.1, f32[]{:T(128)S(6)} %min_shard_map.3, ...), kind=kLoop, calls=%fused_computation.11 | loop fusion | flops 3342336 | bytes 4325380 | tf_op jit(solution)/shard_map/convert_element_type | solution.py:34
  245.2 0.0 copy-done
  245.2 0.0 copy-done.1
  245.2 0.0 copy-done.2
  245.2 0.0 copy-done.3
  245.2 1.1 fusion.8
Async XLA Ops:
  242.0 3.2 %copy-start = (bf16[2,96,512]{2,1,0:T(8,128)(2,1)S(1)}, bf16[2,96,512]{2,1,0:T(8,128)(2,1)}, u32[]{:S(2)}) copy-start(bf16[2,96,512]{2,1,0:T(8,128)(2,1)} %d_in.1) | copy-start | bytes 589828
  242.0 3.2 %copy-start.1 = (f32[2,96,512]{2,1,0:T(8,128)S(1)}, f32[2,96,512]{2,1,0:T(8,128)}, u32[]{:S(2)}) copy-start(f32[2,96,512]{2,1,0:T(8,128)} %param.21) | copy-start | bytes 1179652
  242.0 3.2 %copy-start.2 = (f32[2,96,512]{2,1,0:T(8,128)S(1)}, f32[2,96,512]{2,1,0:T(8,128)}, u32[]{:S(2)}) copy-start(f32[2,96,512]{2,1,0:T(8,128)} %param.18) | copy-start | bytes 1179652
  242.0 3.2 %copy-start.3 = (bf16[2,96,512]{2,1,0:T(8,128)(2,1)S(1)}, bf16[2,96,512]{2,1,0:T(8,128)(2,1)}, u32[]{:S(2)}) copy-start(bf16[2,96,512]{2,1,0:T(8,128)(2,1)} %get-tuple-element.16) | copy-start | bytes 589828

commit v3 on v2

--- a/solution.py
+++ b/solution.py
@@ -13,7 +13,10 @@
 WIDE = 256
 BLOCKS = 3
 CHUNK = WIDE * BLOCKS
+TALL = 512
 ROWS = 256
+EARLY = 2
+WINDOW = 8
 VMEM = pl.BlockSpec(memory_space=pltpu.VMEM)
 HBM = pl.BlockSpec(memory_space=pl.ANY)
 BF16, F32 = jnp.bfloat16, jnp.float32
@@ -58,11 +61,15 @@
     def others(self):
         return [self.partner()] + [self.along(a, k)[1] for a in "xy" for k in range(1, self.side)]
 
+    def slanted(self):
+        return [self.device(self.x, self.along("y", k)[0], 1 - self.c) for k in range(1, self.side)]
+
     def barrier(self):
         sem = pltpu.get_barrier_semaphore()
-        for other in self.others():
+        everyone = self.others() + self.slanted()
+        for other in everyone:
             pl.semaphore_signal(sem, inc=1, device_id=other, device_id_type=MESH)
-        pl.semaphore_wait(sem, len(self.others()))
+        pl.semaphore_wait(sem, len(everyone))
 
 
 def send(src, dst, sems, device):
@@ -72,8 +79,6 @@
 
 
 class Gather:
-    STAGES = 5
-
     def __init__(self, place, whole, rows, cols, send_sems, recv_sems, first):
         p = place
         sems = [(send_sems.at[i], recv_sems.at[i]) for i in range(9)]
@@ -145,14 +150,14 @@
         _, _, paired, _, lined, _ = self.refs
         if stage == 0:
 
-            @pl.loop(0, s * s)
+            @pl.loop(0, s * s, unroll=4)
             def _(i):
                 x, y = i // s, lax.rem(i, s)
                 paired[x, y] = self._pair_sum(x, y).astype(BF16)
 
         else:
 
-            @pl.loop(0, s)
+            @pl.loop(0, s, unroll=True)
             def _(i):
                 lined[i] = self._line_sum(i).astype(BF16)
 
@@ -222,7 +227,7 @@
         _, _, paired, _, lined, _ = self.refs
         if stage == 0:
 
-            @pl.loop(0, self.s)
+            @pl.loop(0, self.s, unroll=True)
             def _(y):
                 paired[y] = self._pair_sum(y).astype(BF16)
 
@@ -249,18 +254,17 @@
 
 def reduced(p, total, squares, others, send_sems, recv_sems):
     at = 0
-    for stage, devices in enumerate(
-        ([p.partner()], [p.along("y", k)[1] for k in range(1, p.side)], [p.along("x", k)[1] for k in range(1, p.side)])
-    ):
+    along = lambda axis: [p.along(axis, k)[1] for k in range(1, p.side)]
+    for stage, devices in enumerate(([p.partner()] + along("y") + p.slanted(), along("x"))):
         squares[stage] = total
         copies = []
         for device in devices:
-            copies.append(send(squares.at[stage], others.at[at], (send_sems.at[at], recv_sems.at[at]), device))
+            copies.append((squares.at[stage], others.at[at], (send_sems.at[at], recv_sems.at[at]), device))
             at += 1
         for copy in copies:
-            copy.start()
+            send(*copy).start()
         for copy in copies:
-            copy.wait()
+            send(*copy).wait()
         for i in range(at - len(copies), at):
             total = total + others[i]
     return total
@@ -270,12 +274,13 @@
     return lax.rsqrt(jnp.mean(wide * wide, -1, keepdims=True) + 1e-6)
 
 
-def kernel(side, x_in, dy_in, g_in, u_in, d_in, og, ou, od, norm, *scratch):
-    (wg, wu, wd, a, a_t, b, b_t, h, acc, p3, squares, others, gg, gu, gd, pg, pu, pd, sg, su, sd, lg, lu, ld, mg, mu, md, eg, eu, ed) = scratch[:30]
-    ag_send, ag_recv, rs_send, rs_recv, local, norm_send, norm_recv, free = scratch[30:]
+def kernel(side, count, x_in, dy_in, g_in, u_in, d_in, *refs):
+    outs, (wg, wu, wd, a, a_t, b, b_t, h, acc, p3, squares, others), refs = refs[:3], refs[3:15], refs[15:]
+    (gg, gu, gd, pg, pu, pd, sg, su, sd, lg, lu, ld, mg, mu, md, eg, eu, ed), refs = refs[:18], refs[18:]
+    ag_send, ag_recv, rs_send, rs_recv, local, norm_send, norm_recv, free = refs
     p = Place(side)
-    layers, depth, hidden = wg.shape[0], a.shape[1], wg.shape[-1]
-    tokens = a.shape[0]
+    layers, tokens, depth = a.shape
+    hidden = wg.shape[-1]
     chunks = hidden // CHUNK
     steps = layers * chunks
     flat_g, flat_u = (w.reshape(layers, depth, hidden) for w in (wg, wu))
@@ -300,7 +305,7 @@
     def pair(*units):
         made = []
         for whole, rows, cols, first in units:
-            at = 2 * len(pairs) + len(made)
+            at = 2 * (len(pairs) % WINDOW) + len(made)
             made.append(Gather(p, whole, rows, cols, ag_send.at[at], ag_recv.at[at], first))
         pairs.append(made)
 
@@ -320,21 +325,20 @@
         if n == layers - 1:
             down_pairs(n)
         for j in range(chunks):
-            if n < layers - 1 and j == chunks - 1:
+            if n < layers - 1 and j == chunks // 2:
                 down_pairs(n)
             chunk_pair(n, j)
 
+    begins = [0, 1, 1, 2, 2, *range(3, len(pairs) - 2)]
+    ends = [begin + len(units[0].stages) for begin, units in zip(begins, pairs)]
+
     def gather_round(r):
-        if r < len(pairs):
-            for unit in pairs[r]:
-                unit.start(0)
-        for stage in range(Gather.STAGES):
-            i = r - 1 - stage
-            if 0 <= i < len(pairs):
-                for unit in pairs[i]:
-                    unit.wait(stage)
-                    if stage + 1 < Gather.STAGES:
-                        unit.start(stage + 1)
+        for begin, end, units in reversed(list(zip(begins, ends, pairs))):
+            for unit in units:
+                if begin < r <= end:
+                    unit.wait(r - begin - 1)
+                if begin <= r < end:
+                    unit.start(r - begin)
 
     def columns(j, n=None):
         if n is None:
@@ -346,51 +350,55 @@
         def _(t):
             body(pl.ds(pl.multiple_of(t * size, size), size))
 
+    bands = [pl.ds(i, TALL) for i in range(0, tokens, TALL)]
+
     def forward(n, j, slot):
-        @pl.loop(0, BLOCKS)
-        def _(i):
-            gate, up = dot(a[...], flat_g[n, :, columns(j, i)]), dot(a[...], flat_u[n, :, columns(j, i)])
-            p3[slot, :, columns(0, i)] = (jax.nn.silu(gate) * up).astype(BF16)
+        for i in range(BLOCKS):
+            for rows in bands:
+                gate, up = dot(a[n, rows, :], flat_g[n, :, columns(j, i)]), dot(a[n, rows, :], flat_u[n, :, columns(j, i)])
+                p3[slot, rows, columns(0, i)] = (jax.nn.silu(gate) * up).astype(BF16)
 
     def down(n, parts, more):
-        @pl.loop(0, depth // WIDE)
-        def _(i):
+        for i in range(depth // WIDE):
             cols = columns(0, i)
-            y = sum(dot(p3[slot], flat_d[n, pl.ds(j * CHUNK, CHUNK), cols]) for j, slot in parts)
-            if more:
-                acc[:, cols] = y
-            else:
-                y = (acc[:, cols] + y).astype(BF16)
-                h[:, cols] = h[:, cols] + y
-
-    def norms(transposed):
+            for rows in bands:
+                y = sum(dot(p3[slot, rows, :], flat_d[n, pl.ds(j * CHUNK, CHUNK), cols]) for j, slot in parts)
+                if more:
+                    acc[rows, cols] = y
+                else:
+                    y = (acc[rows, cols] + y).astype(BF16)
+                    h[rows, cols] = h[rows, cols] + y
+
+    def norms(n):
         def body(rows):
             wide = h[rows, :].astype(F32)
             scaled = (wide * rms(wide)).astype(BF16)
-            a[rows, :] = scaled
-            if transposed:
-                a_t[:, rows] = scaled.T
+            a[n, rows, :] = scaled
+            a_t[n, :, rows] = scaled.T
 
         tiles(ROWS, body)
 
     def transpose_b(rows):
         b_t[:, rows] = b[rows, :].T
 
-    def backward(n, j, i):
-        gate, up = dot(a[...], flat_g[n, :, columns(j, i)]), dot(a[...], flat_u[n, :, columns(j, i)])
-        by_z = dot_t(b[...], flat_d[n, columns(j, i), :]).astype(BF16).astype(F32)
-        s = jax.nn.sigmoid(gate)
-        silu = gate * s
-        cols = columns(0, i)
-        p3[0, :, cols] = (silu * up).astype(BF16)
-        p3[1, :, cols] = (by_z * up * (s + silu * (1 - s))).astype(BF16)
-        p3[2, :, cols] = (by_z * silu).astype(BF16)
+    def backward(n, j):
+        for i in range(BLOCKS):
+            for rows in bands:
+                gate, up = dot(a[n, rows, :], flat_g[n, :, columns(j, i)]), dot(a[n, rows, :], flat_u[n, :, columns(j, i)])
+                by_z = dot_t(b[rows, :], flat_d[n, columns(j, i), :]).astype(BF16).astype(F32)
+                s = jax.nn.sigmoid(gate)
+                silu = gate * s
+                cols = columns(0, i)
+                p3[0, rows, cols] = (silu * up).astype(BF16)
+                p3[1, rows, cols] = (by_z * up * (s + silu * (1 - s))).astype(BF16)
+                p3[2, rows, cols] = (by_z * silu).astype(BF16)
 
     def by_normed(n, j):
-        @pl.loop(0, depth // WIDE)
-        def _(i):
-            rows = columns(0, i)
-            acc[:, rows] += dot_t(p3[1], flat_g[n, rows, columns(j)]) + dot_t(p3[2], flat_u[n, rows, columns(j)])
+        for i in range(depth // WIDE):
+            cols = columns(0, i)
+            for rows in bands:
+                by_gate, by_up = dot_t(p3[1, rows, :], flat_g[n, cols, columns(j)]), dot_t(p3[2, rows, :], flat_u[n, cols, columns(j)])
+                acc[rows, cols] += by_gate + by_up
 
     def by_states(rows):
         wide = h[rows, :].astype(F32)
@@ -419,12 +427,13 @@
 
         def keep(out, *where):
             def write(total):
-                out[where] = total
                 wide = total.astype(F32)
+                out[where] = wide
                 squares[3] = squares[3] + fold(wide * wide)
 
             return write
 
+        og, ou, od = outs
         for unit, write in ((g, keep(og, n, slice(None), columns(j))), (u, keep(ou, n, slice(None), columns(j))), (d, keep(od, n))):
             unit.wait(2)
             unit.result(write)
@@ -437,99 +446,126 @@
     p.barrier()
     for copy in shards():
         copy.wait()
-    last_rounds = Gather.STAGES - 2
-    rounds = len(pairs) + Gather.STAGES
-    done = 0
-    for r in range(rounds - last_rounds):
+    starts = ends[len(pairs) - chunks]
+    half = chunks // 2
+
+    def last_down():
+        down(0, [(j, j - half + 1) for j in range(half, chunks)], False)
+        norms(1)
+        acc[...] = jnp.zeros_like(acc)
+
+    queue = [(j, functools.partial(forward, 0, j, j)) for j in range(half)]
+    queue += [(half + 1, functools.partial(down, 0, [(j, j) for j in range(half)], True))]
+    queue += [(j + 2, functools.partial(forward, 0, j, j - half + 1)) for j in range(half, chunks)]
+    queue += [(chunks + 1, last_down)]
+    work, at = {}, -1
+    for needs, piece in queue:
+        at = max(at + 1, ends[needs])
+        work[at] = piece
+    starts = max(starts, at)
+    for r in range(starts + 1):
         gather_round(r)
         if r == 0:
             load(0).wait()
-            norms(False)
+            norms(0)
         elif r == 1:
             load(1).wait()
             tiles(ROWS, transpose_b)
             squares[3] = jnp.zeros_like(squares[3])
-        ready = r - Gather.STAGES
-        if 0 <= ready < chunks - 1:
-            forward(0, ready, ready)
-        elif ready == chunks:
-            down(0, [(j, j) for j in range(chunks - 1)], True)
-        elif ready == chunks + 1:
-            forward(0, chunks - 1, 0)
-            down(0, [(chunks - 1, 0)], False)
-            norms(True)
-            acc[...] = jnp.zeros_like(acc)
+        if r in work:
+            work[r]()
+
+    def by_weights(n, slot):
+        by_gate, by_up = dot(a_t[n], p3[1]), dot(a_t[n], p3[2])
+        flat_gg[slot] = by_gate.astype(BF16)
+        flat_gu[slot] = by_up.astype(BF16)
+
+    def by_down(slot):
+        flat_gd[slot] = dot(b_t[...], p3[0]).T.astype(BF16)
+
+    def advance(units, stage):
+        for unit in units:
+            unit.wait(stage)
+            unit.add(stage)
+            unit.start(stage + 1)
+
+    def rs0(q):
+        advance(scatters(q)[:2], 0)
+
+    def rs1(q):
+        g, u, d = scatters(q)
+        advance((g, u), 1)
+
+    def rs3(q):
+        advance(scatters(q)[2:], 1)
+
+    def rs2(q):
+        advance(scatters(q)[2:], 0)
+
+    def transition():
+        tiles(ROWS, by_states)
 
     @pl.loop(0, steps + 2)
     def _(q):
         n, j, slot = layers - 1 - q // chunks, lax.rem(q, chunks), lax.rem(q, 2)
         computes = q < steps
-        sends = (q > 0) & (q <= steps)
+        follows = (q > 0) & (q <= steps)
 
         @pl.when(q == chunks)
         def _():
-            tiles(ROWS, by_states)
-            load(0).start()
-            load(0).wait()
-            norms(True)
+            transition()
 
         @pl.when(computes)
         def _():
-            backward(n, j, 0)
-
-        @pl.when(sends)
-        def _():
-            for unit in scatters(q - 1):
-                unit.wait(0)
-                unit.add(0)
-                unit.start(1)
+            backward(n, j)
+
+        @pl.when(follows)
+        def _():
+            rs0(q - 1)
 
         @pl.when(q >= 2)
         def _():
             finish(q - 2)
 
-        @pl.when(computes)
-        def _():
-            @pl.loop(1, BLOCKS)
-            def _(i):
-                backward(n, j, i)
-
-        for k in range(last_rounds):
+        @pl.when(computes & (q < chunks))
+        def _():
+            by_normed(n, j)
+
+        for k in range(ends[-1] - starts):
 
             @pl.when(q == k)
             def _():
-                gather_round(rounds - last_rounds + k)
-
-        @pl.when(computes & (q < chunks))
-        def _():
-            by_normed(n, j)
+                gather_round(starts + 1 + k)
 
         @pl.when(computes)
         def _():
-            g, u, _ = scatters(q)
-            flat_gg[slot] = dot(a_t[...], p3[1]).astype(BF16)
+            by_down(slot)
 
             @pl.when(q >= 2)
             def _():
                 pl.semaphore_wait(free.at[slot], len(p.others()))
 
-            g.start(0)
-            flat_gu[slot] = dot(a_t[...], p3[2]).astype(BF16)
-            u.start(0)
-
-        @pl.when(sends)
-        def _():
-            for unit in scatters(q - 1):
-                unit.wait(1)
-                unit.add(1)
-                unit.start(2)
+            scatters(q)[2].start(0)
+
+        @pl.when(follows)
+        def _():
+            rs3(q - 1)
 
         @pl.when(computes)
         def _():
-            flat_gd[slot] = dot(b_t[...], p3[0]).T.astype(BF16)
-            scatters(q)[2].start(0)
-
-    norm[...] = reduced(p, squares[3], squares, others, norm_send, norm_recv)
+            by_weights(n, slot)
+            for unit in scatters(q)[:2]:
+                unit.start(0)
+            rs2(q)
+
+        @pl.when(follows)
+        def _():
+            rs1(q - 1)
+
+    total = jnp.sum(reduced(p, squares[3], squares, others, norm_send, norm_recv), keepdims=True)
+    factor = jnp.minimum(1.0, 0.5 * lax.rsqrt(total / count + 1e-30))
+    for out in outs:
+        out[...] = out[...] * factor.reshape(1, 1, 1)
 
 
 def gradients_of(side, x, dy, weights):
@@ -545,25 +581,27 @@
     def buffers(lead, lead_d):
         return [pltpu.VMEM(lead + chunk, BF16)] * 2 + [pltpu.VMEM(lead_d + block, BF16)]
 
-    pairs = layers * (hidden // CHUNK + 2)
     stages = 2 * side - 1
+    sums = 3 * side - 2
+    count = side * side * CORES * sum(w.size for w in weights)
     return pl.pallas_call(
-        functools.partial(kernel, side),
-        out_shape=[jax.ShapeDtypeStruct(w.shape, BF16) for w in weights] + [jax.ShapeDtypeStruct((8, 128), F32)],
+        functools.partial(kernel, side, count),
+        out_shape=[jax.ShapeDtypeStruct(w.shape, F32) for w in weights],
         in_specs=[HBM] * 5,
-        out_specs=[VMEM] * 4,
+        out_specs=[VMEM] * 3,
         scratch_shapes=[whole(w) for w in weights]
         + [
-            pltpu.VMEM((tokens, depth), BF16),
-            pltpu.VMEM((depth, tokens), BF16),
+            pltpu.VMEM((layers, tokens, depth), BF16),
+            pltpu.VMEM((layers, depth, tokens), BF16),
             pltpu.VMEM((tokens, depth), BF16),
             pltpu.VMEM((depth, tokens), BF16),
             pltpu.VMEM((tokens, depth), BF16),
             pltpu.VMEM((tokens, depth), F32),
             pltpu.VMEM((3, tokens, CHUNK), BF16),
             pltpu.VMEM((4, 8, 128), F32),
-            pltpu.VMEM((stages, 8, 128), F32),
+            pltpu.VMEM((sums, 8, 128), F32),
         ]
+
         + buffers((2, side, side, CORES), (2, side, CORES))
         + buffers((2, side, side), (2, side))
         + buffers((side, side), (side,))
@@ -571,13 +609,13 @@
         + buffers((side,), ())
         + buffers((2, rest), (2, rest))
         + [
-            pltpu.SemaphoreType.DMA((2 * pairs, 9)),
-            pltpu.SemaphoreType.DMA((2 * pairs, 9)),
+            pltpu.SemaphoreType.DMA((2 * WINDOW, 9)),
+            pltpu.SemaphoreType.DMA((2 * WINDOW, 9)),
             pltpu.SemaphoreType.DMA((2, 3, stages)),
             pltpu.SemaphoreType.DMA((2, 3, stages)),
             pltpu.SemaphoreType.DMA((3 * layers + 2,)),
-            pltpu.SemaphoreType.DMA((stages,)),
-            pltpu.SemaphoreType.DMA((stages,)),
+            pltpu.SemaphoreType.DMA((sums,)),
+            pltpu.SemaphoreType.DMA((sums,)),
             pltpu.SemaphoreType.REGULAR((2,)),
         ],
         compiler_params=pltpu.CompilerParams(collective_id=0, has_side_effects=True, vmem_limit_bytes=67043328),
@@ -590,10 +628,8 @@
 
     def step(x, dy, *arrays):
         weights, m, v = (arrays[i : i + 3] for i in (0, 3, 6))
-        *gradients, squares = gradients_of(side, x, dy, weights)
-        count = mesh.shape["dp"] * sum(g.size for g in gradients)
-        factor = jnp.minimum(1.0, 0.5 * lax.rsqrt(jnp.sum(squares) / count + 1e-30))
-        new = [adamw(w.astype(F32), m, v, g.astype(F32) * factor) for w, m, v, g in zip(weights, m, v, gradients, strict=True)]
+        gradients = gradients_of(side, x, dy, weights)
+        new = [adamw(w.astype(F32), m, v, g) for w, m, v, g in zip(weights, m, v, gradients, strict=True)]
         return tuple(one[which] for which in range(3) for one in new)
 
     states, cut = P(("rep", "dp"), None, None), P(None, "dp", None)

time: 246 us -> 210 us (0.85)
  Pallas kernels: 239 us -> 205 us
    pallas_call x1, Pallas kernels: 239 us -> 205 us  [gradients_of(): pl.pallas_call(functools.partial(kernel, side, count), out_shape=[jax.Sha...]
where the time goes in v3:
time: 210 us
  Pallas kernels  205 us (98%)
  other arithmetic  4.29 us (2%)
    pallas_call x1, Pallas kernels, gradients_of(): pl.pallas_call(functools.partial(kernel, side, count), out_shape=[jax.Sha...  205 us
    convert_element_type x2, other arithmetic, adamw(): return ((w - 0.02 * step).astype(BF16), m, v)  4.29 us

profile of v3, /device:TPU:97, one launch (start us, length us, event | category | flops | bytes accessed | tf_op | source)
XLA Modules:
  0.0 209.9 jit_solution(17616449892390694436)
XLA Ops:
  0.6 204.9 %gradients.1 = (f32[2,16,3072]{2,1,0:T(8,128)}, f32[2,16,3072]{2,1,0:T(8,128)}, f32[2,96,512]{2,1,0:T(8,128)}) custom-call(bf16[1,2048,512]{2,1,0:T(8,128)(2,1)} %x_in.1, bf16[1,2048,512]{2,1,0:T(8,128)(2,1)} %dy_in.1, bf16[2,16,3072]{2,1,0:T(8,128)(2,1)} %g_in.1, bf16[2,16,3072]{2,1,0:T(8,128)(2,1)} %u_in.1, bf16[2,96,512]{2,1,0:T(8,128)(2,1)} %d_in.1), custom_call_target="tpu_custom_call" | custom-call | tf_op jit(solution)/shard_map/gradients/pallas_call | solution.py:587
  205.6 0.0 copy-start
  205.6 0.0 copy-start.1
  205.6 0.0 copy-start.2
  205.6 0.0 copy-start.3
  205.6 3.2 %fusion.2 = (bf16[2,16,3072]{2,1,0:T(8,128)(2,1)}, f32[2,16,3072]{2,1,0:T(8,128)}, f32[2,16,3072]{2,1,0:T(8,128)}, bf16[2,16,3072]{2,1,0:T(8,128)(2,1)}, f32[2,16,3072]{2,1,0:T(8,128)}, /*index=5*/f32[2,16,3072]{2,1,0:T(8,128)}) fusion(bf16[2,16,3072]{2,1,0:T(8,128)(2,1)} %g_in.1, f32[2,16,3072]{2,1,0:T(8,128)} %get-tuple-element.12, ...), kind=kLoop, calls=%fused_computation.11 | loop fusion | flops 2949120 | bytes 4718592 | tf_op jit(solution)/shard_map/convert_element_type | solution.py:37
  208.9 0.0 copy-done
  208.9 0.0 copy-done.1
  208.9 0.0 copy-done.2
  208.9 0.0 copy-done.3
  208.9 1.1 fusion.8
Async XLA Ops:
  205.6 3.3 %copy-start = (bf16[2,96,512]{2,1,0:T(8,128)(2,1)S(1)}, bf16[2,96,512]{2,1,0:T(8,128)(2,1)}, u32[]{:S(2)}) copy-start(bf16[2,96,512]{2,1,0:T(8,128)(2,1)} %d_in.1) | copy-start | bytes 589828
  205.6 3.3 %copy-start.1 = (f32[2,96,512]{2,1,0:T(8,128)S(1)}, f32[2,96,512]{2,1,0:T(8,128)}, u32[]{:S(2)}) copy-start(f32[2,96,512]{2,1,0:T(8,128)} %param.21) | copy-start | bytes 1179652
  205.6 3.3 %copy-start.2 = (f32[2,96,512]{2,1,0:T(8,128)S(1)}, f32[2,96,512]{2,1,0:T(8,128)}, u32[]{:S(2)}) copy-start(f32[2,96,512]{2,1,0:T(8,128)} %param.18) | copy-start | bytes 1179652
  205.6 3.3 %copy-start.3 = (f32[2,96,512]{2,1,0:T(8,128)S(1)}, f32[2,96,512]{2,1,0:T(8,128)}, u32[]{:S(2)}) copy-start(f32[2,96,512]{2,1,0:T(8,128)} %get-tuple-element.14) | copy-start | bytes 1179652

commit v4 on v3

--- a/solution.py
+++ b/solution.py
@@ -13,6 +13,8 @@
 WIDE = 256
 BLOCKS = 3
 CHUNK = WIDE * BLOCKS
+GATHER_STEPS = 5
+SCATTER_STEPS = 3
 TALL = 512
 ROWS = 256
 EARLY = 2
@@ -61,15 +63,16 @@
     def others(self):
         return [self.partner()] + [self.along(a, k)[1] for a in "xy" for k in range(1, self.side)]
 
-    def slanted(self):
-        return [self.device(self.x, self.along("y", k)[0], 1 - self.c) for k in range(1, self.side)]
+    def near(self):
+        ys = [self.along("y", k)[0] for k in range(self.side)]
+        return [self.partner()] + [self.device(self.x, y, c) for y in ys[1:] for c in (self.c, 1 - self.c)]
 
     def barrier(self):
         sem = pltpu.get_barrier_semaphore()
-        everyone = self.others() + self.slanted()
-        for other in everyone:
+        greeted = self.near() + [self.along("x", k)[1] for k in range(1, self.side)]
+        for other in greeted:
             pl.semaphore_signal(sem, inc=1, device_id=other, device_id_type=MESH)
-        pl.semaphore_wait(sem, len(everyone))
+        pl.semaphore_wait(sem, len(greeted))
 
 
 def send(src, dst, sems, device):
@@ -81,7 +84,7 @@
 class Gather:
     def __init__(self, place, whole, rows, cols, send_sems, recv_sems, first):
         p = place
-        sems = [(send_sems.at[i], recv_sems.at[i]) for i in range(9)]
+        sems = [(send_sems.at[i], recv_sems.at[i]) for i in range(GATHER_STEPS)]
         second = "y" if first == "x" else "x"
         half = cols.size // 2
         halves = [pl.ds(cols.start, half), pl.ds(cols.start + half, half)]
@@ -93,21 +96,24 @@
             return whole.at[:, i, p.c, rows, cols] if first == "x" else whole.at[i, :, p.c, rows, cols]
 
         self.stages = []
-        for axis, part, base in ((first, block, 0), (second, line, 4)):
+        both = pl.ds(0, 2)
+        for axis, part in ((first, block), (second, line)):
             me = p.along(axis, 0)[0]
             (after, up), (before, down) = p.along(axis, 1), p.along(axis, -1)
             mine = part(me, cols)
-            self.stages.append([(mine, sems[base], up), (mine, sems[base + 1], down)])
-            self.stages.append([(part(before, halves[0]), sems[base + 2], up), (part(after, halves[1]), sems[base + 3], down)])
-        self.stages.append([(whole.at[:, :, p.c, rows, cols], sems[8], p.partner())])
+            self.stages.append(([(mine, up), (mine, down)], part(both, cols)))
+            self.stages.append(([(part(before, halves[0]), up), (part(after, halves[1]), down)], part(both, halves[0])))
+        plane = whole.at[:, :, p.c, rows, cols]
+        self.stages.append(([(plane, p.partner())], plane))
+        self.sems, self.partner = sems, p.partner()
 
     def start(self, stage):
-        for part, sems, device in self.stages[stage]:
-            send(part, part, sems, device).start()
+        for part, device in self.stages[stage][0]:
+            send(part, part, self.sems[stage], device).start()
 
     def wait(self, stage):
-        for part, sems, device in self.stages[stage]:
-            send(part, part, sems, device).wait()
+        total = self.stages[stage][1]
+        send(total, total, self.sems[stage], self.partner).wait()
 
 
 class Scatter:
@@ -115,24 +121,25 @@
         p, s = place, place.side
         self.p, self.s, self.first, self.refs = p, s, first, refs
         mine, pair, paired, line, lined, last = refs
-        sems = [(send_sems.at[i], recv_sems.at[i]) for i in range(2 * s - 1)]
+        self.sems = [(send_sems.at[i], recv_sems.at[i]) for i in range(SCATTER_STEPS)]
         second = "y" if first == "x" else "x"
-        self.stages = [[(mine.at[:, :, 1 - p.c], pair, sems[0], p.partner())], [], []]
+        self.totals = pair, line, last
+        self.stages = [[(mine.at[:, :, 1 - p.c], pair, p.partner())], [], []]
         for k in range(1, s):
             there, device = p.along(first, k)
             part = paired.at[there] if first == "x" else paired.at[:, there]
-            self.stages[1].append((part, line.at[k - 1], sems[k], device))
+            self.stages[1].append((part, line.at[k - 1], device))
         for k in range(1, s):
             there, device = p.along(second, k)
-            self.stages[2].append((lined.at[there], last.at[k - 1], sems[s - 1 + k], device))
+            self.stages[2].append((lined.at[there], last.at[k - 1], device))
 
     def start(self, stage):
-        for copy in self.stages[stage]:
-            send(*copy).start()
+        for src, dst, device in self.stages[stage]:
+            send(src, dst, self.sems[stage], device).start()
 
     def wait(self, stage):
-        for copy in self.stages[stage]:
-            send(*copy).wait()
+        total = self.totals[stage]
+        send(total, total, self.sems[stage], self.p.partner()).wait()
 
     def _pair_sum(self, x, y):
         mine, pair = self.refs[:2]
@@ -174,23 +181,23 @@
         p, s = place, place.side
         self.p, self.s, self.refs, self.owner = p, s, refs, owner
         mine, pair, paired, line, lined, last = refs
-        sems = [(send_sems.at[i], recv_sems.at[i]) for i in range(2 * s - 1)]
-        self.first = [(mine.at[:, 1 - p.c], pair, sems[0], p.partner())]
+        self.sems = [(send_sems.at[i], recv_sems.at[i]) for i in range(SCATTER_STEPS)]
+        self.totals = pair, line, last
+        self.first = [(mine.at[:, 1 - p.c], pair, p.partner())]
         self.second = []
         for k in range(1, s):
             there, device = p.along("y", k)
-            self.second.append((paired.at[there], line.at[k - 1], sems[k], device))
-        self.last_sems = [sems[s - 1 + k] for k in range(1, s)]
+            self.second.append((paired.at[there], line.at[k - 1], device))
         self.away = lax.rem(owner - p.x + s, s)
 
     def _last(self, k):
         lined, last = self.refs[4:]
-        return send(lined, last.at[k - 1], self.last_sems[k - 1], self.p.device(self.owner, self.p.y, self.p.c))
+        return send(lined, last.at[k - 1], self.sems[2], self.p.device(self.owner, self.p.y, self.p.c))
 
     def start(self, stage):
         if stage < 2:
-            for copy in (self.first, self.second)[stage]:
-                send(*copy).start()
+            for src, dst, device in (self.first, self.second)[stage]:
+                send(src, dst, self.sems[stage], device).start()
         else:
             for k in range(1, self.s):
 
@@ -199,19 +206,19 @@
                     self._last(k).start()
 
     def wait(self, stage):
+        total = self.totals[stage]
+        whole = lambda: send(total, total, self.sems[stage], self.p.partner())
         if stage < 2:
-            for copy in (self.first, self.second)[stage]:
-                send(*copy).wait()
+            whole().wait()
         else:
-            for k in range(1, self.s):
-
-                @pl.when(self.away == k)
-                def _():
-                    self._last(k).wait_send()
-
-                @pl.when(self.away == 0)
-                def _():
-                    self._last(k).wait_recv()
+
+            @pl.when(self.away > 0)
+            def _():
+                self._last(1).wait_send()
+
+            @pl.when(self.away == 0)
+            def _():
+                whole().wait_recv()
 
     def _pair_sum(self, y):
         mine, pair = self.refs[:2]
@@ -252,21 +259,18 @@
     return total
 
 
-def reduced(p, total, squares, others, send_sems, recv_sems):
+def reduced(p, total, mine, others, send_sems, recv_sems):
     at = 0
-    along = lambda axis: [p.along(axis, k)[1] for k in range(1, p.side)]
-    for stage, devices in enumerate(([p.partner()] + along("y") + p.slanted(), along("x"))):
-        squares[stage] = total
-        copies = []
-        for device in devices:
-            copies.append((squares.at[stage], others.at[at], (send_sems.at[at], recv_sems.at[at]), device))
-            at += 1
-        for copy in copies:
-            send(*copy).start()
-        for copy in copies:
-            send(*copy).wait()
-        for i in range(at - len(copies), at):
-            total = total + others[i]
+    for stage, devices in enumerate((p.near(), [p.along("x", k)[1] for k in range(1, p.side)])):
+        sems = send_sems.at[stage], recv_sems.at[stage]
+        mine[stage] = total
+        for i, device in enumerate(devices):
+            send(mine.at[stage], others.at[at + i], sems, device).start()
+        came = others.at[pl.ds(at, len(devices))]
+        send(came, came, sems, p.partner()).wait()
+        for i in range(len(devices)):
+            total = total + others[at + i]
+        at += len(devices)
     return total
 
 
@@ -346,7 +350,7 @@
         return pl.ds(pl.multiple_of(j * CHUNK + n * WIDE, WIDE), WIDE)
 
     def tiles(size, body):
-        @pl.loop(0, tokens // size)
+        @pl.loop(0, tokens // size, unroll=2)
         def _(t):
             body(pl.ds(pl.multiple_of(t * size, size), size))
 
@@ -429,7 +433,7 @@
             def write(total):
                 wide = total.astype(F32)
                 out[where] = wide
-                squares[3] = squares[3] + fold(wide * wide)
+                squares[2] = squares[2] + fold(wide * wide)
 
             return write
 
@@ -471,7 +475,7 @@
         elif r == 1:
             load(1).wait()
             tiles(ROWS, transpose_b)
-            squares[3] = jnp.zeros_like(squares[3])
+            squares[2] = jnp.zeros_like(squares[2])
         if r in work:
             work[r]()
 
@@ -481,7 +485,7 @@
         flat_gu[slot] = by_up.astype(BF16)
 
     def by_down(slot):
-        flat_gd[slot] = dot(b_t[...], p3[0]).T.astype(BF16)
+        flat_gd[slot] = dot(b_t[...], p3[0]).astype(BF16).T
 
     def advance(units, stage):
         for unit in units:
@@ -562,7 +566,7 @@
         def _():
             rs1(q - 1)
 
-    total = jnp.sum(reduced(p, squares[3], squares, others, norm_send, norm_recv), keepdims=True)
+    total = jnp.sum(reduced(p, squares[2], squares, others, norm_send, norm_recv), keepdims=True)
     factor = jnp.minimum(1.0, 0.5 * lax.rsqrt(total / count + 1e-30))
     for out in outs:
         out[...] = out[...] * factor.reshape(1, 1, 1)
@@ -581,7 +585,6 @@
     def buffers(lead, lead_d):
         return [pltpu.VMEM(lead + chunk, BF16)] * 2 + [pltpu.VMEM(lead_d + block, BF16)]
 
-    stages = 2 * side - 1
     sums = 3 * side - 2
     count = side * side * CORES * sum(w.size for w in weights)
     return pl.pallas_call(
@@ -598,7 +601,7 @@
             pltpu.VMEM((tokens, depth), BF16),
             pltpu.VMEM((tokens, depth), F32),
             pltpu.VMEM((3, tokens, CHUNK), BF16),
-            pltpu.VMEM((4, 8, 128), F32),
+            pltpu.VMEM((3, 8, 128), F32),
             pltpu.VMEM((sums, 8, 128), F32),
         ]
 
@@ -609,13 +612,13 @@
         + buffers((side,), ())
         + buffers((2, rest), (2, rest))
         + [
-            pltpu.SemaphoreType.DMA((2 * WINDOW, 9)),
-            pltpu.SemaphoreType.DMA((2 * WINDOW, 9)),
-            pltpu.SemaphoreType.DMA((2, 3, stages)),
-            pltpu.SemaphoreType.DMA((2, 3, stages)),
+            pltpu.SemaphoreType.DMA((2 * WINDOW, GATHER_STEPS)),
+            pltpu.SemaphoreType.DMA((2 * WINDOW, GATHER_STEPS)),
+            pltpu.SemaphoreType.DMA((2, 3, SCATTER_STEPS)),
+            pltpu.SemaphoreType.DMA((2, 3, SCATTER_STEPS)),
             pltpu.SemaphoreType.DMA((3 * layers + 2,)),
-            pltpu.SemaphoreType.DMA((sums,)),
-            pltpu.SemaphoreType.DMA((sums,)),
+            pltpu.SemaphoreType.DMA((2,)),
+            pltpu.SemaphoreType.DMA((2,)),
             pltpu.SemaphoreType.REGULAR((2,)),
         ],
         compiler_params=pltpu.CompilerParams(collective_id=0, has_side_effects=True, vmem_limit_bytes=67043328),

time: 210 us -> 207 us (0.986)
  Pallas kernels: 205 us -> 202 us
    pallas_call x1, Pallas kernels: 205 us -> 202 us  [gradients_of(): pl.pallas_call(functools.partial(kernel, side, count), out_shape=[jax.Sha...]
where the time goes in v4:
time: 207 us
  Pallas kernels  202 us (98%)
  other arithmetic  4.29 us (2%)
    pallas_call x1, Pallas kernels, gradients_of(): pl.pallas_call(functools.partial(kernel, side, count), out_shape=[jax.Sha...  202 us
    convert_element_type x2, other arithmetic, adamw(): return ((w - 0.02 * step).astype(BF16), m, v)  4.29 us

profile of v4, /device:TPU:97, one launch (start us, length us, event | category | flops | bytes accessed | tf_op | source)
XLA Modules:
  0.0 206.9 jit_solution(7147044337706296676)
XLA Ops:
  0.6 201.9 %gradients.1 = (f32[2,16,3072]{2,1,0:T(8,128)}, f32[2,16,3072]{2,1,0:T(8,128)}, f32[2,96,512]{2,1,0:T(8,128)}) custom-call(bf16[1,2048,512]{2,1,0:T(8,128)(2,1)} %x_in.1, bf16[1,2048,512]{2,1,0:T(8,128)(2,1)} %dy_in.1, bf16[2,16,3072]{2,1,0:T(8,128)(2,1)} %g_in.1, bf16[2,16,3072]{2,1,0:T(8,128)(2,1)} %u_in.1, bf16[2,96,512]{2,1,0:T(8,128)(2,1)} %d_in.1), custom_call_target="tpu_custom_call" | custom-call | tf_op jit(solution)/shard_map/gradients/pallas_call | solution.py:590
  202.5 0.0 copy-start
  202.6 0.0 copy-start.1
  202.6 0.0 copy-start.2
  202.6 0.0 copy-start.3
  202.6 3.2 %fusion.2 = (bf16[2,16,3072]{2,1,0:T(8,128)(2,1)}, f32[2,16,3072]{2,1,0:T(8,128)}, f32[2,16,3072]{2,1,0:T(8,128)}, bf16[2,16,3072]{2,1,0:T(8,128)(2,1)}, f32[2,16,3072]{2,1,0:T(8,128)}, /*index=5*/f32[2,16,3072]{2,1,0:T(8,128)}) fusion(bf16[2,16,3072]{2,1,0:T(8,128)(2,1)} %g_in.1, f32[2,16,3072]{2,1,0:T(8,128)} %get-tuple-element.12, ...), kind=kLoop, calls=%fused_computation.11 | loop fusion | flops 2949120 | bytes 4718592 | tf_op jit(solution)/shard_map/convert_element_type | solution.py:39
  205.8 0.0 copy-done
  205.8 0.0 copy-done.1
  205.8 0.0 copy-done.2
  205.9 0.0 copy-done.3
  205.9 1.1 fusion.8
Async XLA Ops:
  202.5 3.3 %copy-start = (bf16[2,96,512]{2,1,0:T(8,128)(2,1)S(1)}, bf16[2,96,512]{2,1,0:T(8,128)(2,1)}, u32[]{:S(2)}) copy-start(bf16[2,96,512]{2,1,0:T(8,128)(2,1)} %d_in.1) | copy-start | bytes 589828
  202.6 3.3 %copy-start.1 = (f32[2,96,512]{2,1,0:T(8,128)S(1)}, f32[2,96,512]{2,1,0:T(8,128)}, u32[]{:S(2)}) copy-start(f32[2,96,512]{2,1,0:T(8,128)} %param.21) | copy-start | bytes 1179652
  202.6 3.3 %copy-start.2 = (f32[2,96,512]{2,1,0:T(8,128)S(1)}, f32[2,96,512]{2,1,0:T(8,128)}, u32[]{:S(2)}) copy-start(f32[2,96,512]{2,1,0:T(8,128)} %param.18) | copy-start | bytes 1179652
  202.6 3.3 %copy-start.3 = (f32[2,96,512]{2,1,0:T(8,128)S(1)}, f32[2,96,512]{2,1,0:T(8,128)}, u32[]{:S(2)}) copy-start(f32[2,96,512]{2,1,0:T(8,128)} %get-tuple-element.14) | copy-start | bytes 1179652

commit v5 on v4

--- a/solution.py
+++ b/solution.py
@@ -333,7 +333,7 @@
                 down_pairs(n)
             chunk_pair(n, j)
 
-    begins = [0, 1, 1, 2, 2, *range(3, len(pairs) - 2)]
+    begins = [0, 1, 1, 2, 2, 3, 3, *range(4, len(pairs) - 3)]
     ends = [begin + len(units[0].stages) for begin, units in zip(begins, pairs)]
 
     def gather_round(r):

time: 207 us -> 211 us (1.019)
  Pallas kernels: 202 us -> 206 us
    pallas_call x1, Pallas kernels: 202 us -> 206 us  [gradients_of(): pl.pallas_call(functools.partial(kernel, side, count), out_shape=[jax.Sha...]
where the time goes in v5:
time: 211 us
  Pallas kernels  206 us (98%)
  other arithmetic  4.29 us (2%)
    pallas_call x1, Pallas kernels, gradients_of(): pl.pallas_call(functools.partial(kernel, side, count), out_shape=[jax.Sha...  206 us
    convert_element_type x2, other arithmetic, adamw(): return ((w - 0.02 * step).astype(BF16), m, v)  4.29 us

profile of v5, /device:TPU:97, one launch (start us, length us, event | category | flops | bytes accessed | tf_op | source)
XLA Modules:
  0.0 210.7 jit_solution(13528394540654800723)
XLA Ops:
  0.6 205.7 %gradients.1 = (f32[2,16,3072]{2,1,0:T(8,128)}, f32[2,16,3072]{2,1,0:T(8,128)}, f32[2,96,512]{2,1,0:T(8,128)}) custom-call(bf16[1,2048,512]{2,1,0:T(8,128)(2,1)} %x_in.1, bf16[1,2048,512]{2,1,0:T(8,128)(2,1)} %dy_in.1, bf16[2,16,3072]{2,1,0:T(8,128)(2,1)} %g_in.1, bf16[2,16,3072]{2,1,0:T(8,128)(2,1)} %u_in.1, bf16[2,96,512]{2,1,0:T(8,128)(2,1)} %d_in.1), custom_call_target="tpu_custom_call" | custom-call | tf_op jit(solution)/shard_map/gradients/pallas_call | solution.py:590
  206.3 0.0 copy-start
  206.4 0.0 copy-start.1
  206.4 0.0 copy-start.2
  206.4 0.0 copy-start.3
  206.4 3.2 %fusion.2 = (bf16[2,16,3072]{2,1,0:T(8,128)(2,1)}, f32[2,16,3072]{2,1,0:T(8,128)}, f32[2,16,3072]{2,1,0:T(8,128)}, bf16[2,16,3072]{2,1,0:T(8,128)(2,1)}, f32[2,16,3072]{2,1,0:T(8,128)}, /*index=5*/f32[2,16,3072]{2,1,0:T(8,128)}) fusion(bf16[2,16,3072]{2,1,0:T(8,128)(2,1)} %g_in.1, f32[2,16,3072]{2,1,0:T(8,128)} %get-tuple-element.12, ...), kind=kLoop, calls=%fused_computation.11 | loop fusion | flops 2949120 | bytes 4718592 | tf_op jit(solution)/shard_map/convert_element_type | solution.py:39
  209.6 0.0 copy-done
  209.6 0.0 copy-done.1
  209.6 0.0 copy-done.2
  209.7 0.0 copy-done.3
  209.7 1.1 fusion.8
Async XLA Ops:
  206.3 3.3 %copy-start = (bf16[2,96,512]{2,1,0:T(8,128)(2,1)S(1)}, bf16[2,96,512]{2,1,0:T(8,128)(2,1)}, u32[]{:S(2)}) copy-start(bf16[2,96,512]{2,1,0:T(8,128)(2,1)} %d_in.1) | copy-start | bytes 589828
  206.4 3.3 %copy-start.1 = (f32[2,96,512]{2,1,0:T(8,128)S(1)}, f32[2,96,512]{2,1,0:T(8,128)}, u32[]{:S(2)}) copy-start(f32[2,96,512]{2,1,0:T(8,128)} %param.21) | copy-start | bytes 1179652
  206.4 3.3 %copy-start.2 = (f32[2,96,512]{2,1,0:T(8,128)S(1)}, f32[2,96,512]{2,1,0:T(8,128)}, u32[]{:S(2)}) copy-start(f32[2,96,512]{2,1,0:T(8,128)} %param.18) | copy-start | bytes 1179652
  206.4 3.3 %copy-start.3 = (f32[2,96,512]{2,1,0:T(8,128)S(1)}, f32[2,96,512]{2,1,0:T(8,128)}, u32[]{:S(2)}) copy-start(f32[2,96,512]{2,1,0:T(8,128)} %get-tuple-element.14) | copy-start | bytes 1179652
